TPU v7x, 16 devices: a whole 2x2x2 slice. The times are simulated.
16 devices in a mesh: rep: 1, dp: 16 (over x, y, z, core).
Axes of the slice: x: 2, y: 2, z: 2, core: 2. Of those that a mesh axis runs over, the one named last changes fastest.
Arguments:
- x: bfloat16 [16, 2048, 896], P(('rep', 'dp'))
- dy: bfloat16 [16, 2048, 896], P(('rep', 'dp'))
- w_gate: bfloat16 [2, 896, 3584], replicated
- w_up: bfloat16 [2, 896, 3584], replicated
- w_down: bfloat16 [2, 3584, 896], replicated
- m_w_gate: float32 [2, 896, 3584], P(None, 'dp')
- m_w_up: float32 [2, 896, 3584], P(None, 'dp')
- m_w_down: float32 [2, 3584, 896], P(None, 'dp')
- v_w_gate: float32 [2, 896, 3584], P(None, 'dp')
- v_w_up: float32 [2, 896, 3584], P(None, 'dp')
- v_w_down: float32 [2, 3584, 896], P(None, 'dp')
Outputs:
- output 1: bfloat16 [2, 896, 3584], P('rep')
- output 2: bfloat16 [2, 896, 3584], P('rep')
- output 3: bfloat16 [2, 3584, 896], P('rep')
- output 4: float32 [2, 896, 3584], P('rep', 'dp')
- output 5: float32 [2, 896, 3584], P('rep', 'dp')
- output 6: float32 [2, 3584, 896], P('rep', 'dp')
- output 7: float32 [2, 896, 3584], P('rep', 'dp')
- output 8: float32 [2, 896, 3584], P('rep', 'dp')
- output 9: float32 [2, 3584, 896], P('rep', 'dp')
All inputs are finite; a program needn't handle non-finite values.
Results may differ from a plain program's by a relative error of at most 0.022.
Values are sent between devices in bfloat16 or wider.
A program may use at most 2 GiB of HBM per device.

v0:
```python
import functools

import jax
import jax.numpy as jnp
from jax import lax
from jax.experimental import pallas as pl
from jax.experimental.pallas import tpu as pltpu
from jax.sharding import PartitionSpec as P


BF, F32 = jnp.bfloat16, jnp.float32
CORE = 1
BIT = {"x": 8, "y": 4, "z": 2}
VMEM = 60 * 2**20


def dot(a, b, ca, cb):
    return lax.dot_general(a, b, (((ca,), (cb,)), ((), ())), preferred_element_type=F32)


def call(kernel, grid, ins, outs, shapes, flops, scratch=(), prefetch=0, aliases={}):
    spec = pltpu.PrefetchScalarGridSpec(
        num_scalar_prefetch=prefetch, grid=grid, in_specs=ins, out_specs=outs, scratch_shapes=scratch
    )
    return pl.pallas_call(
        kernel,
        grid_spec=spec,
        out_shape=shapes,
        input_output_aliases=aliases,
        cost_estimate=pl.CostEstimate(flops=flops, bytes_accessed=flops // 400, transcendentals=0),
        compiler_params=pltpu.CompilerParams(
            vmem_limit_bytes=VMEM, dimension_semantics=("arbitrary",) * len(grid)
        ),
    )


def like(*shapes):
    return [jax.ShapeDtypeStruct(s, d) for s, d in shapes]


def scale_of(wide):
    return lax.rsqrt(jnp.mean(wide**2, -1, keepdims=True) + 1e-6)


def normed(h):
    wide = h.astype(F32)
    return (wide * scale_of(wide)).astype(BF)


def forward(a, w_gate, w_up, n, tile=512):
    t, d = a.shape
    ff = w_gate.shape[2]

    def kernel(a, wg, wu, gate, up, hid):
        g = dot(a[...], wg[...], 1, 0)
        u = dot(a[...], wu[...], 1, 0)
        gate[...] = g
        up[...] = u
        hid[...] = (g * sigmoid(g) * u).astype(BF)

    w = pl.BlockSpec((None, d, tile), lambda j: (n, 0, j))
    o = pl.BlockSpec((t, tile), lambda j: (0, j))
    return call(
        kernel,
        (ff // tile,),
        [pl.BlockSpec((t, d), lambda j: (0, 0)), w, w],
        [o, o, o],
        like(((t, ff), F32), ((t, ff), F32), ((t, ff), BF)),
        4 * t * d * ff,
    )(a, w_gate, w_up)


def down(x, hid, w_down, n, tile=512):
    t, d = x.shape
    ff = hid.shape[1]

    def kernel(x, hid, w, h, a):
        new = x[...].astype(F32) + dot(hid[...], w[...], 1, 0).astype(BF).astype(F32)
        new = new.astype(BF)
        h[...] = new
        a[...] = normed(new)

    o = pl.BlockSpec((tile, d), lambda i: (i, 0))
    return call(
        kernel,
        (t // tile,),
        [o, pl.BlockSpec((tile, ff), lambda i: (i, 0)), pl.BlockSpec((None, ff, d), lambda i: (n, 0, 0))],
        [o, o],
        like(((t, d), BF), ((t, d), BF)),
        2 * t * d * ff,
    )(x, hid, w_down)


def sigmoid(x):
    return 0.5 * jnp.tanh(0.5 * x) + 0.5


def gated_back(g, u, d_hid):
    d_hid = d_hid.astype(BF).astype(F32)
    s = sigmoid(g)
    act = g * s
    d_up = (d_hid * act).astype(BF)
    d_gate = (d_hid * u * (s + act * (1 - s))).astype(BF)
    return act, d_gate, d_up


def turn(a, back, w_gate, w_up, w_down, n, tile=256):
    t, d = a.shape
    ff = w_gate.shape[2]

    def kernel(a, back, wg, wu, wd, hid, d_gate, d_up):
        for r in range(0, t, 512):
            r = slice(r, r + 512)
            g = dot(a[r], wg[...], 1, 0)
            u = dot(a[r], wu[...], 1, 0)
            act, d_gate[r], d_up[r] = gated_back(g, u, dot(back[r], wd[...], 1, 1))
            hid[r] = (act * u).astype(BF)

    whole = pl.BlockSpec((t, d), lambda j: (0, 0))
    w = pl.BlockSpec((None, d, tile), lambda j: (n, 0, j))
    o = pl.BlockSpec((t, tile), lambda j: (0, j))
    return call(
        kernel,
        (ff // tile,),
        [whole, whole, w, w, pl.BlockSpec((None, tile, d), lambda j: (n, j, 0))],
        [o, o, o],
        like(*[((t, ff), BF)] * 3),
        6 * t * d * ff,
    )(a, back, w_gate, w_up, w_down)


def backward(back, gate, up, w_down, n, first, steps, onto=(), tile=512):
    t, d = back.shape
    ff = gate.shape[1]

    def kernel(back, wd, g, u, *refs):
        d_gate, d_up = refs[-2:]
        _, d_gate[...], d_up[...] = gated_back(g[...], u[...], dot(back[...], wd[...], 1, 1))

    o = pl.BlockSpec((t, tile), lambda j: (0, first + j))
    return call(
        kernel,
        (steps,),
        [
            pl.BlockSpec((t, d), lambda j: (0, 0)),
            pl.BlockSpec((None, tile, d), lambda j: (n, first + j, 0)),
            o,
            o,
            *[pl.BlockSpec(memory_space=pl.ANY) for _ in onto],
        ],
        [o, o],
        like(*[((t, ff), BF)] * 2),
        2 * t * d * tile * steps,
        aliases={4: 0, 5: 1} if onto else {},
    )(back, w_down, gate, up, *onto)


def through(d_gate, d_up, w_gate, w_up, h, back, n, half, onto=None, tile=512):
    t, d = h.shape
    ff = d_gate.shape[1]

    def kernel(dg, du, wg, wu, h, back, *refs):
        out = refs[-1]
        d_a = dot(dg[...], wg[...], 1, 1).astype(BF).astype(F32) + dot(du[...], wu[...], 1, 1).astype(BF).astype(F32)
        d_a = d_a.astype(BF).astype(F32)
        wide = h[...].astype(F32)
        scale = scale_of(wide)
        along = jnp.mean(d_a * wide, -1, keepdims=True)
        d_h = scale * d_a - wide * (scale**3 * along)
        out[...] = (back[...].astype(F32) + d_h.astype(BF).astype(F32)).astype(BF)

    steps = t // tile // 2
    o = pl.BlockSpec((tile, d), lambda i: (i + half * steps, 0))
    wide = pl.BlockSpec((tile, ff), lambda i: (i + half * steps, 0))
    w = pl.BlockSpec((None, d, ff), lambda i: (n, 0, 0))
    more = [] if onto is None else [onto]
    return call(
        kernel,
        (steps,),
        [wide, wide, w, w, o, o, *[pl.BlockSpec(memory_space=pl.ANY) for _ in more]],
        o,
        like(((t, d), BF))[0],
        2 * t * d * ff,
        aliases={6: 0} if more else {},
    )(d_gate, d_up, w_gate, w_up, h, back, *more)


def by_columns(me, a, b, tile=512):
    t, d = a.shape
    ff = b.shape[1]
    rows = d // 16

    def kernel(me, a, b, keep, send, acc):
        acc[...] = dot(a[...], b[...], 0, 0).reshape(acc.shape)
        for j in range(8):
            keep[j] = acc[(2 * j) ^ me[0]].astype(BF)
            send[j] = acc[(2 * j + 1) ^ me[0]].astype(BF)

    o = pl.BlockSpec((8, rows, tile), lambda j, me: (0, 0, j))
    return call(
        kernel,
        (ff // tile,),
        [pl.BlockSpec((t, d), lambda j, me: (0, 0)), pl.BlockSpec((t, tile), lambda j, me: (0, j))],
        [o, o],
        like(*[((8, rows, ff), BF)] * 2),
        2 * t * d * ff,
        scratch=[pltpu.VMEM((16, rows, tile), F32)],
        prefetch=1,
    )(me, a, b)


def by_rows(me, a, b):
    t, ff = a.shape
    d = b.shape[1]
    rows = ff // 16

    def kernel(me, a, b, keep, send, acc):
        acc[...] = dot(a[...], b[...], 0, 0).reshape(acc.shape)
        low = me[0] & 3
        for j in range(2):
            keep[j] = acc[(2 * j) ^ low].astype(BF)
            send[j] = acc[(2 * j + 1) ^ low].astype(BF)

    o = pl.BlockSpec((2, rows, d), lambda i, me: (i ^ (me[0] >> 2), 0, 0))
    return call(
        kernel,
        (4,),
        [pl.BlockSpec((t, ff // 4), lambda i, me: (0, i)), pl.BlockSpec((t, d), lambda i, me: (0, 0))],
        [o, o],
        like(*[((8, rows, d), BF)] * 2),
        2 * t * d * ff,
        scratch=[pltpu.VMEM((4, rows, d), F32)],
        prefetch=1,
    )(me, a, b)


def swap(t, bit):
    return lax.ppermute(t, "dp", [(i, i ^ bit) for i in range(16)])


def add(terms):
    return functools.reduce(jnp.add, [t.astype(F32) for t in terms]).astype(BF)


def scattered(keep, send, pieces):
    got = swap(send, CORE)
    out = []
    for start, stop, order in pieces:
        terms = [t.reshape(2, 2, 2, *t.shape[1:])[..., start:stop] for t in (keep, got)]
        left = "xyz"
        for axis in order:
            k = left.index(axis)
            left = left.replace(axis, "")
            near, far = ([lax.index_in_dim(t, side, k, keepdims=False) for t in terms] for side in (0, 1))
            sent = add(far)
            terms = [*near, swap(sent, BIT[axis])]
        out.append(add(terms))
    return out


def gathered(block, order):
    held = block[None]
    for axis in reversed(order):
        got = swap(held, BIT[axis])
        held = jnp.concatenate([held, got])
    return held, swap(held, CORE)


def put(full, n, layers, onto):
    rows, width = full.shape[0] // 16, full.shape[1]

    def kernel(full, *refs):
        refs[-1][...] = full[...]

    more = [] if onto is None else [onto]
    return call(
        kernel,
        (4,),
        [pl.BlockSpec((2, 2, rows, width), lambda k: (k, 0, 0, 0)), *[pl.BlockSpec(memory_space=pl.ANY) for _ in more]],
        pl.BlockSpec((None, 2, 2, rows, width), lambda k: (n, k, 0, 0, 0)),
        like(((layers, 8, 2, rows, width), BF))[0],
        10**9,
        aliases={1: 0} if more else {},
    )(full.reshape(8, 2, rows, width), *more)


def placed(parts, pieces, n, onto):
    _, _, _, rows, width = onto.shape
    flat = [t for both in parts for t in both]

    def kernel(*refs):
        out, held, came, went = refs[-4:]
        me = lax.axis_index("dp")
        core, pair = me & 1, me >> 1

        def copies(j):
            bits = {"x": j >> 2, "y": (j >> 1) & 1, "z": j & 1}
            k = pair ^ j
            for i, (start, stop, order) in enumerate(pieces):
                at = bits[order[0]] * 4 + bits[order[1]] * 2 + bits[order[2]]
                for side in range(2):
                    yield pltpu.make_async_copy(
                        refs[2 * i + side].at[at],
                        held.at[k, core ^ side, :, start:stop],
                        came.at[j, 2 * i + side],
                    )

        def leave(j):
            k = pair ^ j
            return pltpu.make_async_copy(held.at[k], out.at[n, k], went.at[j])

        for j in range(8):
            for copy in copies(j):
                copy.start()
        for j in range(8):
            for copy in copies(j):
                copy.wait()
            leave(j).start()
        for j in range(8):
            leave(j).wait()

    whole = pl.BlockSpec(memory_space=pl.ANY)
    return pl.pallas_call(
        kernel,
        in_specs=[whole] * (len(flat) + 1),
        out_specs=whole,
        out_shape=jax.ShapeDtypeStruct(onto.shape, BF),
        input_output_aliases={len(flat): 0},
        scratch_shapes=[
            pltpu.VMEM((8, 2, rows, width), BF),
            pltpu.SemaphoreType.DMA((8, 2 * len(parts))),
            pltpu.SemaphoreType.DMA((8,)),
        ],
        cost_estimate=pl.CostEstimate(flops=10**9, bytes_accessed=10**7, transcendentals=0),
        compiler_params=pltpu.CompilerParams(vmem_limit_bytes=VMEM),
        name="placed",
    )(*flat, onto)


def adamw(w, m, v, g):
    m = 0.9 * m + 0.1 * g
    v = 0.95 * v + 0.05 * g * g
    step = m * lax.rsqrt(v + 1e-8) + 0.1 * w
    return (w - 0.02 * step).astype(BF), m, v


def solution(mesh):
    ORDERS = ("xyz", "yzx", "zxy")

    def body(x, dy, w_gate, w_up, w_down, *moments):
        x, dy = x[0], dy[0]
        m, v = moments[:3], moments[3:]
        me = lax.axis_index("dp")
        at = me.astype(jnp.int32)[None]
        weights = (w_gate, w_up, w_down)
        new = [[None] * 2 for _ in range(9)]
        whole = [None] * 3

        def pieces_of(which, n):
            width = weights[which].shape[2]
            if n == 1:
                return [(0, width, ORDERS[which])]
            cuts = [0, 1152, 2304, 3584] if width == 3584 else [0, 256, 512, 896]
            return [(cuts[i], cuts[i + 1], ORDERS[(which + i) % 3]) for i in range(3)]

        def update(which, n, keep, send):
            pieces = pieces_of(which, n)
            g = scattered(keep, send, pieces)
            rows = weights[which].shape[1] // 16
            parts, ms, vs = [], [], []
            for (start, stop, order), g in zip(pieces, g, strict=True):
                width = stop - start
                w = lax.dynamic_slice(weights[which], (n, me * rows, start), (1, rows, width))[0].astype(F32)
                w, m2, v2 = adamw(w, m[which][n, :, start:stop], v[which][n, :, start:stop], g.astype(F32))
                ms.append(m2)
                vs.append(v2)
                parts.append(w if n else gathered(w, order))
            new[3 + which][n] = jnp.concatenate(ms, -1)
            new[6 + which][n] = jnp.concatenate(vs, -1)
            if n:
                got = lax.all_gather(parts[0], "dp", axis=0, tiled=True)
                whole[which] = put(got, n, 2, None)
            else:
                whole[which] = placed(parts, pieces, n, whole[which])

        a0 = normed(x)
        gate, up, hid0 = forward(a0, w_gate, w_up, 0)
        h, a1 = down(x, hid0, w_down, 0)
        hid1, d_gate, d_up = turn(a1, dy, w_gate, w_up, w_down, 1)
        update(2, 1, *by_rows(at, hid1, dy))
        update(0, 1, *by_columns(at, a1, d_gate))
        update(1, 1, *by_columns(at, a1, d_up))
        back = through(d_gate, d_up, w_gate, w_up, h, dy, 1, 0)
        back = through(d_gate, d_up, w_gate, w_up, h, dy, 1, 1, back)
        update(2, 0, *by_rows(at, hid0, back))
        d_both = backward(back, gate, up, w_down, 0, 0, 4)
        d_gate, d_up = backward(back, gate, up, w_down, 0, 4, 3, d_both)
        update(0, 0, *by_columns(at, a0, d_gate))
        update(1, 0, *by_columns(at, a0, d_up))
        for i in range(3):
            new[i] = whole[i].reshape(weights[i].shape)
        return tuple(one if i < 3 else jnp.stack(one) for i, one in enumerate(new))

    seq = P(("rep", "dp"), None, None)
    full = P(None, None, None)
    block = P(None, "dp", None)
    return jax.shard_map(
        body,
        mesh=mesh,
        in_specs=(seq, seq, *[full] * 3, *[block] * 6),
        out_specs=(*[P("rep", None, None)] * 3, *[P("rep", "dp", None)] * 6),
        check_vma=False,
    )
```

profile of v0, /device:TPU:0, one launch (start us, length us, event | category | flops | bytes accessed | tf_op | source)
XLA Modules:
  0.0 751.8 jit_solution(4417117237987851953)
XLA Ops:
  7.2 3.0 fusion
  10.4 2.5 fusion.1.a
  12.9 40.2 %shard_map.178 = (f32[2048,3584]{1,0:T(8,128)}, f32[2048,3584]{1,0:T(8,128)}, bf16[2048,3584]{1,0:T(8,128)(2,1)}) custom-call(bf16[2048,896]{1,0:T(8,128)(2,1)} %fusion.1.a, bf16[2,896,3584]{2,1,0:T(8,128)(2,1)} %wg.7, bf16[2,896,3584]{2,1,0:T(8,128)(2,1)} %wu.7), custom_call_target="tpu_custom_call" | custom-call | flops 26306674688 | bytes 65766688 | tf_op jit(solution)/shard_map/pallas_call | solution.py:63
  53.1 22.5 %shard_map.179 = (bf16[2048,896]{1,0:T(8,128)(2,1)}, bf16[2048,896]{1,0:T(8,128)(2,1)}) custom-call(bf16[2048,896]{1,0:T(8,128)(2,1)} %bitcast.673, bf16[2048,3584]{1,0:T(8,128)(2,1)} %get-tuple-element.33.hid.a, bf16[2,3584,896]{2,1,0:T(8,128)(2,1)} %wd.5), custom_call_target="tpu_custom_call" | custom-call | flops 13153337344 | bytes 32883344 | tf_op jit(solution)/shard_map/pallas_call | solution.py:84
  75.5 54.5 %shard_map.180 = (bf16[2048,3584]{1,0:T(8,128)(2,1)}, bf16[2048,3584]{1,0:T(8,128)(2,1)}, bf16[2048,3584]{1,0:T(8,128)(2,1)}) custom-call(bf16[2048,896]{1,0:T(8,128)(2,1)} %get-tuple-element.34.a, bf16[2048,896]{1,0:T(8,128)(2,1)} %bitcast.674, bf16[2,896,3584]{2,1,0:T(8,128)(2,1)} %wg.7, bf16[2,896,3584]{2,1,0:T(8,128)(2,1)} %wu.7, bf16[2,3584,896]{2,1,0:T(8,128)(2,1)} %wd.5), custom_call_target="tpu_custom_call" | custom-call | flops 39460012032 | bytes 98650032 | tf_op jit(solution)/shard_map/pallas_call | solution.py:122
  130.0 21.4 %shard_map.192 = (bf16[8,224,896]{2,1,0:T(8,128)(2,1)}, bf16[8,224,896]{2,1,0:T(8,128)(2,1)}) custom-call(s32[1]{0:T(128)} %bitcast.2.me, bf16[2048,3584]{1,0:T(8,128)(2,1)} %get-tuple-element.54.a, bf16[2048,896]{1,0:T(8,128)(2,1)} %bitcast.675), custom_call_target="tpu_custom_call" | custom-call | flops 13153337344 | bytes 32883344 | tf_op jit(solution)/shard_map/pallas_call | solution.py:225
  152.2 26.6 %shard_map.181.refs_0_ = bf16[2048,896]{1,0:T(8,128)(2,1)} custom-call(bf16[2048,3584]{1,0:T(8,128)(2,1)} %get-tuple-element.35.dg.b, bf16[2048,3584]{1,0:T(8,128)(2,1)} %get-tuple-element.36.du.b, bf16[2,896,3584]{2,1,0:T(8,128)(2,1)} %wg.7, bf16[2,896,3584]{2,1,0:T(8,128)(2,1)} %wu.7, bf16[2048,896]{1,0:T(8,128)(2,1)} %get-tuple-element.37.h, ...), custom_call_target="tpu_custom_call" | custom-call | flops 13153337344 | bytes 32883344 | tf_op jit(solution)/shard_map/pallas_call | solution.py:177
  178.8 26.2 %shard_map.182.back.b = bf16[2048,896]{1,0:T(8,128)(2,1)} custom-call(bf16[2048,3584]{1,0:T(8,128)(2,1)} %get-tuple-element.35.dg.b, bf16[2048,3584]{1,0:T(8,128)(2,1)} %get-tuple-element.36.du.b, bf16[2,896,3584]{2,1,0:T(8,128)(2,1)} %wg.7, bf16[2,896,3584]{2,1,0:T(8,128)(2,1)} %wu.7, ...), custom_call_target="tpu_custom_call", output_to_operand_aliasing={{}: (6, {})} | custom-call | flops 13153337344 | bytes 32883344 | tf_op jit(solution)/shard_map/pallas_call | solution.py:177
  205.0 21.5 %shard_map.191 = (bf16[8,224,896]{2,1,0:T(8,128)(2,1)}, bf16[8,224,896]{2,1,0:T(8,128)(2,1)}) custom-call(s32[1]{0:T(128)} %bitcast.2.me, bf16[2048,3584]{1,0:T(8,128)(2,1)} %get-tuple-element.33.hid.a, bf16[2048,896]{1,0:T(8,128)(2,1)} %shard_map.182.back.b), custom_call_target="tpu_custom_call" | custom-call | flops 13153337344 | bytes 32883344 | tf_op jit(solution)/shard_map/pallas_call | solution.py:225
  226.5 26.0 %shard_map.183 = (bf16[2048,3584]{1,0:T(8,128)(2,1)}, bf16[2048,3584]{1,0:T(8,128)(2,1)}) custom-call(bf16[2048,896]{1,0:T(8,128)(2,1)} %shard_map.182.back.b, bf16[2,3584,896]{2,1,0:T(8,128)(2,1)} %wd.5, f32[2048,3584]{1,0:T(8,128)} %get-tuple-element.38.g, f32[2048,3584]{1,0:T(8,128)} %get-tuple-element.39.u), custom_call_target="tpu_custom_call" | custom-call | flops 7516192768 | bytes 18790480 | tf_op jit(solution)/shard_map/pallas_call | solution.py:141
  252.6 22.1 %shard_map.184 = (bf16[2048,3584]{1,0:T(8,128)(2,1)}, bf16[2048,3584]{1,0:T(8,128)(2,1)}) custom-call(bf16[2048,896]{1,0:T(8,128)(2,1)} %shard_map.182.back.b, bf16[2,3584,896]{2,1,0:T(8,128)(2,1)} %wd.5, f32[2048,3584]{1,0:T(8,128)} %get-tuple-element.38.g, f32[2048,3584]{1,0:T(8,128)} %get-tuple-element.39.u, ...), custom_call_target="tpu_custom_call", output_to_operand_aliasing={{0}: (4, {}), {1}: (5, {})} | custom-call | flops 5637144576 | bytes 14092861 | tf_op jit(solution)/shard_map/pallas_call | solution.py:141
  274.7 3.0 fusion.3
  277.7 3.1 collective-permute-start.75
  280.7 19.2 %shard_map.188 = (bf16[8,56,3584]{2,1,0:T(8,128)(2,1)}, bf16[8,56,3584]{2,1,0:T(8,128)(2,1)}) custom-call(s32[1]{0:T(128)} %bitcast.2.me, bf16[2048,896]{1,0:T(8,128)(2,1)} %fusion.1.a, bf16[2048,3584]{1,0:T(8,128)(2,1)} %get-tuple-element.47.b), custom_call_target="tpu_custom_call" | custom-call | flops 13153337344 | bytes 32883344 | tf_op jit(solution)/shard_map/pallas_call | solution.py:200
  299.9 19.0 %shard_map.189 = (bf16[8,56,3584]{2,1,0:T(8,128)(2,1)}, bf16[8,56,3584]{2,1,0:T(8,128)(2,1)}) custom-call(s32[1]{0:T(128)} %bitcast.2.me, bf16[2048,896]{1,0:T(8,128)(2,1)} %get-tuple-element.34.a, bf16[2048,3584]{1,0:T(8,128)(2,1)} %get-tuple-element.36.du.b), custom_call_target="tpu_custom_call" | custom-call | flops 13153337344 | bytes 32883344 | tf_op jit(solution)/shard_map/pallas_call | solution.py:200
  322.7 19.0 %shard_map.185 = (bf16[8,56,3584]{2,1,0:T(8,128)(2,1)}, bf16[8,56,3584]{2,1,0:T(8,128)(2,1)}) custom-call(s32[1]{0:T(128)} %bitcast.2.me, bf16[2048,896]{1,0:T(8,128)(2,1)} %fusion.1.a, bf16[2048,3584]{1,0:T(8,128)(2,1)} %get-tuple-element.42.b), custom_call_target="tpu_custom_call" | custom-call | flops 13153337344 | bytes 32883344 | tf_op jit(solution)/shard_map/pallas_call | solution.py:200
  345.3 19.0 %shard_map.186 = (bf16[8,56,3584]{2,1,0:T(8,128)(2,1)}, bf16[8,56,3584]{2,1,0:T(8,128)(2,1)}) custom-call(s32[1]{0:T(128)} %bitcast.2.me, bf16[2048,896]{1,0:T(8,128)(2,1)} %get-tuple-element.34.a, bf16[2048,3584]{1,0:T(8,128)(2,1)} %get-tuple-element.35.dg.b), custom_call_target="tpu_custom_call" | custom-call | flops 13153337344 | bytes 32883344 | tf_op jit(solution)/shard_map/pallas_call | solution.py:200
  364.6 2.9 fusion.49
  367.4 2.5 fusion.46
  393.4 39.8 %collective-permute-done.49 = bf16[2,2,56,3584]{3,2,1,0:T(8,128)(2,1)S(1)} collective-permute-done((bf16[2,2,56,3584]{3,2,1,0:T(8,128)(2,1)S(1)}, bf16[2,2,56,3584]{3,2,1,0:T(8,128)(2,1)S(1)}, u32[]{:S(2)}, u32[]{:S(2)}) %collective-permute-start.49) | collective-permute-done | bytes 1605664 | tf_op jit(solution)/shard_map/ppermute | solution.py:238
  439.6 13.3 %collective-permute-done.50 = bf16[2,56,3584]{2,1,0:T(8,128)(2,1)S(1)} collective-permute-done((bf16[2,56,3584]{2,1,0:T(8,128)(2,1)S(1)}, bf16[2,56,3584]{2,1,0:T(8,128)(2,1)S(1)}, u32[]{:S(2)}, u32[]{:S(2)}) %collective-permute-start.50) | collective-permute-done | bytes 802848 | tf_op jit(solution)/shard_map/ppermute | solution.py:238
  455.2 7.1 collective-permute-done.51
  464.6 2.5 fusion.47
  479.7 3.9 collective-permute-done.34
  487.2 5.7 collective-permute-done.1
  495.3 2.5 collective-permute-start.23
  497.9 14.0 %collective-permute-done.8 = bf16[2,2,56,1152]{3,2,1,0:T(8,128)(2,1)S(1)} collective-permute-done((bf16[2,2,56,1152]{3,2,1,0:T(8,128)(2,1)S(1)}, bf16[2,2,56,1152]{3,2,1,0:T(8,128)(2,1)S(1)}, u32[]{:S(2)}, u32[]{:S(2)}) %collective-permute-start.8) | collective-permute-done | bytes 516128 | tf_op jit(solution)/shard_map/ppermute | solution.py:238
  513.2 2.9 collective-permute-start.54
  519.9 3.4 collective-permute-done.61
  527.0 24.8 %collective-permute-done.35 = bf16[2,56,1152]{2,1,0:T(8,128)(2,1)S(1)} collective-permute-done((bf16[2,56,1152]{2,1,0:T(8,128)(2,1)S(1)}, bf16[2,56,1152]{2,1,0:T(8,128)(2,1)S(1)}, u32[]{:S(2)}, u32[]{:S(2)}) %collective-permute-start.35) | collective-permute-done | bytes 258080 | tf_op jit(solution)/shard_map/ppermute | solution.py:238
  568.8 8.3 %collective-permute-done.24 = bf16[2,56,3584]{2,1,0:T(8,128)(2,1)S(1)} collective-permute-done((bf16[2,56,3584]{2,1,0:T(8,128)(2,1)S(1)}, bf16[2,56,3584]{2,1,0:T(8,128)(2,1)S(1)}, u32[]{:S(2)}, u32[]{:S(2)}) %collective-permute-start.24) | collective-permute-done | bytes 802848 | tf_op jit(solution)/shard_map/ppermute | solution.py:238
  581.5 7.2 collective-permute-done.25
  591.9 2.5 fusion.48
  613.2 5.8 collective-permute-done.63
  619.4 5.2 collective-permute-done.56
  639.3 6.1 collective-permute-done.64
  649.1 5.6 collective-permute-done.38
  658.9 4.2 collective-permute-done.70
  667.3 5.0 collective-permute-done.65
  672.3 2.5 collective-permute-start.13
  674.9 6.2 collective-permute-done.71
  691.4 5.0 collective-permute-done.46
  707.6 6.0 shard_map.193.refs_6_
  713.7 6.0 shard_map.190.refs_6_
  719.7 6.0 shard_map.187.refs_6_
  725.6 6.0 placed.5
  731.7 6.0 placed.4
  739.1 6.0 placed.3
  (354 shorter events, 163.1 us)
Async XLA Ops:
  7.2 700.5 %all-gather.8.cloned.1.call-start = ((), (), s32[]{:S(2)}) async-start(), calls=%async_computation.2 | async-start | bytes 6823936 | tf_op jit(solution)/shard_map/all_gather | solution.py:381
  151.4 123.2 %collective-permute-start.74 = (bf16[8,224,896]{2,1,0:T(8,128)(2,1)}, bf16[8,224,896]{2,1,0:T(8,128)(2,1)}, u32[]{:S(2)}, u32[]{:S(2)}) collective-permute-start(bf16[8,224,896]{2,1,0:T(8,128)(2,1)} %get-tuple-element.56), channel_id=1, source_target_pairs={{0,1},{1,0},{2,3},{3,2},{4,5},{5,4},{6,7},{7,6},{8,9},{9,8},{10,11... | collective-permute-start | bytes 9633800 | tf_op jit(solution)/shard_map/ppermute | solution.py:238
  226.5 152.3 %collective-permute-start.52 = (bf16[8,224,896]{2,1,0:T(8,128)(2,1)}, bf16[8,224,896]{2,1,0:T(8,128)(2,1)}, u32[]{:S(2)}, u32[]{:S(2)}) collective-permute-start(bf16[8,224,896]{2,1,0:T(8,128)(2,1)} %get-tuple-element.53), channel_id=1, source_target_pairs={{0,1},{1,0},{2,3},{3,2},{4,5},{5,4},{6,7},{7,6},{8,9},{9,8},{10,11... | collective-permute-start | bytes 9633800 | tf_op jit(solution)/shard_map/ppermute | solution.py:238
  277.7 41.8 %collective-permute-start.75 = (bf16[2,2,224,896]{3,2,1,0:T(8,128)(2,1)}, bf16[2,2,224,896]{3,2,1,0:T(8,128)(2,1)}, u32[]{:S(2)}, u32[]{:S(2)}) collective-permute-start(bf16[2,2,224,896]{3,2,1,0:T(8,128)(2,1)} %fusion.3), channel_id=1, source_target_pairs={{0,2},{1,3},{2,0},{3,1},{4,6},{5,7},{6,4},{7,5},{8,10},{9,11},{10,... | collective-permute-start | bytes 4816904 | tf_op jit(solution)/shard_map/ppermute | solution.py:238
  299.9 82.1 %collective-permute-start.26 = (bf16[8,56,3584]{2,1,0:T(8,128)(2,1)}, bf16[8,56,3584]{2,1,0:T(8,128)(2,1)}, u32[]{:S(2)}, u32[]{:S(2)}) collective-permute-start(bf16[8,56,3584]{2,1,0:T(8,128)(2,1)} %get-tuple-element.49), channel_id=1, source_target_pairs={{0,1},{1,0},{2,3},{3,2},{4,5},{5,4},{6,7},{7,6},{8,9},{9,8},{10,11... | collective-permute-start | bytes 9633800 | tf_op jit(solution)/shard_map/ppermute | solution.py:238
  319.0 57.1 %collective-permute-start.48 = (bf16[8,56,3584]{2,1,0:T(8,128)(2,1)}, bf16[8,56,3584]{2,1,0:T(8,128)(2,1)}, u32[]{:S(2)}, u32[]{:S(2)}) collective-permute-start(bf16[8,56,3584]{2,1,0:T(8,128)(2,1)} %get-tuple-element.51), channel_id=1, source_target_pairs={{0,1},{1,0},{2,3},{3,2},{4,5},{5,4},{6,7},{7,6},{8,9},{9,8},{10,11... | collective-permute-start | bytes 9633800 | tf_op jit(solution)/shard_map/ppermute | solution.py:238
  321.1 20.6 %collective-permute-start.76 = (bf16[2,224,896]{2,1,0:T(8,128)(2,1)S(1)}, bf16[2,224,896]{2,1,0:T(8,128)(2,1)}, u32[]{:S(2)}, u32[]{:S(2)}) collective-permute-start(bf16[2,224,896]{2,1,0:T(8,128)(2,1)S(1)} %fusion.4), channel_id=1, source_target_pairs={{0,8},{1,9},{2,10},{3,11},{4,12},{5,13},{6,14},{7,15},{8,0},{9,1},... | collective-permute-start | bytes 2408456 | tf_op jit(solution)/shard_map/ppermute | solution.py:238
  341.7 92.6 %collective-permute-start = (bf16[8,56,3584]{2,1,0:T(8,128)(2,1)}, bf16[8,56,3584]{2,1,0:T(8,128)(2,1)}, u32[]{:S(2)}, u32[]{:S(2)}) collective-permute-start(bf16[8,56,3584]{2,1,0:T(8,128)(2,1)} %get-tuple-element.44), channel_id=1, source_target_pairs={{0,1},{1,0},{2,3},{3,2},{4,5},{5,4},{6,7},{7,6},{8,9},{9,8},{10,11... | collective-permute-start | bytes 9633800 | tf_op jit(solution)/shard_map/ppermute | solution.py:238
  343.9 20.4 %collective-permute-start.77 = (bf16[224,896]{1,0:T(8,128)(2,1)}, bf16[224,896]{1,0:T(8,128)(2,1)}, u32[]{:S(2)}, u32[]{:S(2)}) collective-permute-start(bf16[224,896]{1,0:T(8,128)(2,1)} %fusion.22), channel_id=1, source_target_pairs={{0,4},{1,5},{2,6},{3,7},{4,0},{5,1},{6,2},{7,3},{8,12},{9,13},{10,... | collective-permute-start | bytes 1204232 | tf_op jit(solution)/shard_map/ppermute | solution.py:238
  364.3 103.3 %collective-permute-start.22 = (bf16[8,56,3584]{2,1,0:T(8,128)(2,1)}, bf16[8,56,3584]{2,1,0:T(8,128)(2,1)}, u32[]{:S(2)}, u32[]{:S(2)}) collective-permute-start(bf16[8,56,3584]{2,1,0:T(8,128)(2,1)} %get-tuple-element.46), channel_id=1, source_target_pairs={{0,1},{1,0},{2,3},{3,2},{4,5},{5,4},{6,7},{7,6},{8,9},{9,8},{10,11... | collective-permute-start | bytes 9633800 | tf_op jit(solution)/shard_map/ppermute | solution.py:238
  369.9 343.7 %all-gather.6.cloned.1.call-start = ((), (), s32[]{:S(2)}) async-start(), calls=%async_computation.1 | async-start | bytes 6823936 | tf_op jit(solution)/shard_map/all_gather | solution.py:381
  378.0 55.2 %collective-permute-start.49 = (bf16[2,2,56,3584]{3,2,1,0:T(8,128)(2,1)S(1)}, bf16[2,2,56,3584]{3,2,1,0:T(8,128)(2,1)S(1)}, u32[]{:S(2)}, u32[]{:S(2)}) collective-permute-start(bf16[2,2,56,3584]{3,2,1,0:T(8,128)(2,1)S(1)} %fusion.2), channel_id=1, source_target_pairs={{0,4},{1,5},{2,6},{3,7},{4,0},{5,1},{6,2},{7,3},{8,12},{9,13},{10,... | collective-permute-start | bytes 4816904 | tf_op jit(solution)/shard_map/ppermute | solution.py:238
  388.0 130.8 %collective-permute-start.67 = (bf16[2,2,224,384]{3,2,1,0:T(8,128)(2,1)S(1)}, bf16[2,2,224,384]{3,2,1,0:T(8,128)(2,1)S(1)}, u32[]{:S(2)}, u32[]{:S(2)}) collective-permute-start(bf16[2,2,224,384]{3,2,1,0:T(8,128)(2,1)S(1)} %fusion.31), channel_id=1, source_target_pairs={{0,4},{1,5},{2,6},{3,7},{4,0},{5,1},{6,2},{7,3},{8,12},{9,13},{10,... | collective-permute-start | bytes 2064392 | tf_op jit(solution)/shard_map/ppermute | solution.py:238
  389.3 86.4 %collective-permute-start.53 = (bf16[2,2,224,256]{3,2,1,0:T(8,128)(2,1)}, bf16[2,2,224,256]{3,2,1,0:T(8,128)(2,1)}, u32[]{:S(2)}, u32[]{:S(2)}) collective-permute-start(bf16[2,2,224,256]{3,2,1,0:T(8,128)(2,1)} %fusion.42), channel_id=1, source_target_pairs={{0,2},{1,3},{2,0},{3,1},{4,6},{5,7},{6,4},{7,5},{8,10},{9,11},{10,... | collective-permute-start | bytes 1376264 | tf_op jit(solution)/shard_map/ppermute | solution.py:238
  433.2 43.2 %collective-permute-start.60 = (bf16[2,2,224,256]{3,2,1,0:T(8,128)(2,1)}, bf16[2,2,224,256]{3,2,1,0:T(8,128)(2,1)}, u32[]{:S(2)}, u32[]{:S(2)}) collective-permute-start(bf16[2,2,224,256]{3,2,1,0:T(8,128)(2,1)} %fusion.43), channel_id=1, source_target_pairs={{0,8},{1,9},{2,10},{3,11},{4,12},{5,13},{6,14},{7,15},{8,0},{9,1},... | collective-permute-start | bytes 1376264 | tf_op jit(solution)/shard_map/ppermute | solution.py:238
  434.3 18.6 %collective-permute-start.50 = (bf16[2,56,3584]{2,1,0:T(8,128)(2,1)S(1)}, bf16[2,56,3584]{2,1,0:T(8,128)(2,1)S(1)}, u32[]{:S(2)}, u32[]{:S(2)}) collective-permute-start(bf16[2,56,3584]{2,1,0:T(8,128)(2,1)S(1)} %fusion.21), channel_id=1, source_target_pairs={{0,2},{1,3},{2,0},{3,1},{4,6},{5,7},{6,4},{7,5},{8,10},{9,11},{10,... | collective-permute-start | bytes 2408456 | tf_op jit(solution)/shard_map/ppermute | solution.py:238
  462.4 50.8 %collective-permute-start.41 = (bf16[2,2,56,1280]{3,2,1,0:T(8,128)(2,1)}, bf16[2,2,56,1280]{3,2,1,0:T(8,128)(2,1)}, u32[]{:S(2)}, u32[]{:S(2)}) collective-permute-start(bf16[2,2,56,1280]{3,2,1,0:T(8,128)(2,1)} %fusion.33), channel_id=1, source_target_pairs={{0,8},{1,9},{2,10},{3,11},{4,12},{5,13},{6,14},{7,15},{8,0},{9,1},... | collective-permute-start | bytes 1720328 | tf_op jit(solution)/shard_map/ppermute | solution.py:238
  467.1 252.5 %all-gather.4.cloned.1.call-start = ((), (), s32[]{:S(2)}) async-start(), calls=%async_computation | async-start | bytes 6823936 | tf_op jit(solution)/shard_map/all_gather | solution.py:381
  475.7 19.6 %collective-permute-start.27 = (bf16[2,2,56,1152]{3,2,1,0:T(8,128)(2,1)S(1)}, bf16[2,2,56,1152]{3,2,1,0:T(8,128)(2,1)S(1)}, u32[]{:S(2)}, u32[]{:S(2)}) collective-permute-start(bf16[2,2,56,1152]{3,2,1,0:T(8,128)(2,1)S(1)} %copy-done.44), channel_id=1, source_target_pairs={{0,4},{1,5},{2,6},{3,7},{4,0},{5,1},{6,2},{7,3},{8,12},{9,13},{10,... | collective-permute-start | bytes 1548296 | tf_op jit(solution)/shard_map/ppermute | solution.py:238
  483.6 33.7 %collective-permute-start.15 = (bf16[2,2,56,1280]{3,2,1,0:T(8,128)(2,1)S(1)}, bf16[2,2,56,1280]{3,2,1,0:T(8,128)(2,1)S(1)}, u32[]{:S(2)}, u32[]{:S(2)}) collective-permute-start(bf16[2,2,56,1280]{3,2,1,0:T(8,128)(2,1)S(1)} %copy-done.43), channel_id=1, source_target_pairs={{0,2},{1,3},{2,0},{3,1},{4,6},{5,7},{6,4},{7,5},{8,10},{9,11},{10,... | collective-permute-start | bytes 1720328 | tf_op jit(solution)/shard_map/ppermute | solution.py:238
  492.9 19.1 %collective-permute-start.8 = (bf16[2,2,56,1152]{3,2,1,0:T(8,128)(2,1)S(1)}, bf16[2,2,56,1152]{3,2,1,0:T(8,128)(2,1)S(1)}, u32[]{:S(2)}, u32[]{:S(2)}) collective-permute-start(bf16[2,2,56,1152]{3,2,1,0:T(8,128)(2,1)S(1)} %copy-done.45), channel_id=1, source_target_pairs={{0,4},{1,5},{2,6},{3,7},{4,0},{5,1},{6,2},{7,3},{8,12},{9,13},{10,... | collective-permute-start | bytes 1548296 | tf_op jit(solution)/shard_map/ppermute | solution.py:238
  495.3 61.7 %collective-permute-start.23 = (bf16[2,2,56,3584]{3,2,1,0:T(8,128)(2,1)S(1)}, bf16[2,2,56,3584]{3,2,1,0:T(8,128)(2,1)S(1)}, u32[]{:S(2)}, u32[]{:S(2)}) collective-permute-start(bf16[2,2,56,3584]{3,2,1,0:T(8,128)(2,1)S(1)} %bitcast.715), channel_id=1, source_target_pairs={{0,8},{1,9},{2,10},{3,11},{4,12},{5,13},{6,14},{7,15},{8,0},{9,1},... | collective-permute-start | bytes 4816904 | tf_op jit(solution)/shard_map/ppermute | solution.py:238
  513.2 48.4 %collective-permute-start.54 = (bf16[2,224,256]{2,1,0:T(8,128)(2,1)S(1)}, bf16[2,224,256]{2,1,0:T(8,128)(2,1)S(1)}, u32[]{:S(2)}, u32[]{:S(2)}) collective-permute-start(bf16[2,224,256]{2,1,0:T(8,128)(2,1)S(1)} %get-tuple-element.102), channel_id=1, source_target_pairs={{0,8},{1,9},{2,10},{3,11},{4,12},{5,13},{6,14},{7,15},{8,0},{9,1},... | collective-permute-start | bytes 688136 | tf_op jit(solution)/shard_map/ppermute | solution.py:238
  518.8 33.1 %collective-permute-start.35 = (bf16[2,56,1152]{2,1,0:T(8,128)(2,1)S(1)}, bf16[2,56,1152]{2,1,0:T(8,128)(2,1)S(1)}, u32[]{:S(2)}, u32[]{:S(2)}) collective-permute-start(bf16[2,56,1152]{2,1,0:T(8,128)(2,1)S(1)} %fusion.40), channel_id=1, source_target_pairs={{0,8},{1,9},{2,10},{3,11},{4,12},{5,13},{6,14},{7,15},{8,0},{9,1},... | collective-permute-start | bytes 774152 | tf_op jit(solution)/shard_map/ppermute | solution.py:238
  523.3 31.7 %collective-permute-start.9 = (bf16[2,56,1152]{2,1,0:T(8,128)(2,1)S(1)}, bf16[2,56,1152]{2,1,0:T(8,128)(2,1)S(1)}, u32[]{:S(2)}, u32[]{:S(2)}) collective-permute-start(bf16[2,56,1152]{2,1,0:T(8,128)(2,1)S(1)} %fusion.97), channel_id=1, source_target_pairs={{0,2},{1,3},{2,0},{3,1},{4,6},{5,7},{6,4},{7,5},{8,10},{9,11},{10,... | collective-permute-start | bytes 774152 | tf_op jit(solution)/shard_map/ppermute | solution.py:238
  525.5 33.7 %collective-permute-start.2 = (bf16[2,56,1152]{2,1,0:T(8,128)(2,1)S(1)}, bf16[2,56,1152]{2,1,0:T(8,128)(2,1)S(1)}, u32[]{:S(2)}, u32[]{:S(2)}) collective-permute-start(bf16[2,56,1152]{2,1,0:T(8,128)(2,1)S(1)} %fusion.41), channel_id=1, source_target_pairs={{0,4},{1,5},{2,6},{3,7},{4,0},{5,1},{6,2},{7,3},{8,12},{9,13},{10,... | collective-permute-start | bytes 774152 | tf_op jit(solution)/shard_map/ppermute | solution.py:238
  554.9 24.4 %collective-permute-start.16 = (bf16[2,56,1280]{2,1,0:T(8,128)(2,1)S(1)}, bf16[2,56,1280]{2,1,0:T(8,128)(2,1)S(1)}, u32[]{:S(2)}, u32[]{:S(2)}) collective-permute-start(bf16[2,56,1280]{2,1,0:T(8,128)(2,1)S(1)} %fusion.35), channel_id=1, source_target_pairs={{0,8},{1,9},{2,10},{3,11},{4,12},{5,13},{6,14},{7,15},{8,0},{9,1},... | collective-permute-start | bytes 860168 | tf_op jit(solution)/shard_map/ppermute | solution.py:238
  559.2 17.8 %collective-permute-start.24 = (bf16[2,56,3584]{2,1,0:T(8,128)(2,1)S(1)}, bf16[2,56,3584]{2,1,0:T(8,128)(2,1)S(1)}, u32[]{:S(2)}, u32[]{:S(2)}) collective-permute-start(bf16[2,56,3584]{2,1,0:T(8,128)(2,1)S(1)} %fusion.5), channel_id=1, source_target_pairs={{0,4},{1,5},{2,6},{3,7},{4,0},{5,1},{6,2},{7,3},{8,12},{9,13},{10,... | collective-permute-start | bytes 2408456 | tf_op jit(solution)/shard_map/ppermute | solution.py:238
  561.6 49.2 %collective-permute-start.68 = (bf16[2,224,384]{2,1,0:T(8,128)(2,1)}, bf16[2,224,384]{2,1,0:T(8,128)(2,1)}, u32[]{:S(2)}, u32[]{:S(2)}) collective-permute-start(bf16[2,224,384]{2,1,0:T(8,128)(2,1)} %fusion.57), channel_id=1, source_target_pairs={{0,2},{1,3},{2,0},{3,1},{4,6},{5,7},{6,4},{7,5},{8,10},{9,11},{10,... | collective-permute-start | bytes 1032200 | tf_op jit(solution)/shard_map/ppermute | solution.py:238
  562.8 31.6 %collective-permute-start.29 = (bf16[56,1152]{1,0:T(8,128)(2,1)}, bf16[56,1152]{1,0:T(8,128)(2,1)}, u32[]{:S(2)}, u32[]{:S(2)}) collective-permute-start(bf16[56,1152]{1,0:T(8,128)(2,1)} %fusion.102), channel_id=1, source_target_pairs={{0,8},{1,9},{2,10},{3,11},{4,12},{5,13},{6,14},{7,15},{8,0},{9,1},... | collective-permute-start | bytes 387080 | tf_op jit(solution)/shard_map/ppermute | solution.py:238
  565.6 30.3 %collective-permute-start.36 = (bf16[56,1152]{1,0:T(8,128)(2,1)}, bf16[56,1152]{1,0:T(8,128)(2,1)}, u32[]{:S(2)}, u32[]{:S(2)}) collective-permute-start(bf16[56,1152]{1,0:T(8,128)(2,1)} %fusion.99), channel_id=1, source_target_pairs={{0,4},{1,5},{2,6},{3,7},{4,0},{5,1},{6,2},{7,3},{8,12},{9,13},{10,... | collective-permute-start | bytes 387080 | tf_op jit(solution)/shard_map/ppermute | solution.py:238
  577.1 22.3 %collective-permute-start.10 = (bf16[56,1152]{1,0:T(8,128)(2,1)}, bf16[56,1152]{1,0:T(8,128)(2,1)}, u32[]{:S(2)}, u32[]{:S(2)}) collective-permute-start(bf16[56,1152]{1,0:T(8,128)(2,1)} %fusion.105), channel_id=1, source_target_pairs={{0,8},{1,9},{2,10},{3,11},{4,12},{5,13},{6,14},{7,15},{8,0},{9,1},... | collective-permute-start | bytes 387080 | tf_op jit(solution)/shard_map/ppermute | solution.py:238
  599.7 26.4 %collective-permute-start.37 = (bf16[1,56,1152]{2,1,0:T(8,128)(2,1)S(1)}, bf16[1,56,1152]{2,1,0:T(8,128)(2,1)S(1)}, u32[]{:S(2)}, u32[]{:S(2)}) collective-permute-start(bf16[1,56,1152]{2,1,0:T(8,128)(2,1)S(1)} %get-tuple-element.75), channel_id=1, source_target_pairs={{0,4},{1,5},{2,6},{3,7},{4,0},{5,1},{6,2},{7,3},{8,12},{9,13},{10,... | collective-permute-start | bytes 387080 | tf_op jit(solution)/shard_map/ppermute | solution.py:238
  603.2 23.5 %collective-permute-start.30 = (bf16[1,56,1152]{2,1,0:T(8,128)(2,1)S(1)}, bf16[1,56,1152]{2,1,0:T(8,128)(2,1)S(1)}, u32[]{:S(2)}, u32[]{:S(2)}) collective-permute-start(bf16[1,56,1152]{2,1,0:T(8,128)(2,1)S(1)} %get-tuple-element.93), channel_id=1, source_target_pairs={{0,8},{1,9},{2,10},{3,11},{4,12},{5,13},{6,14},{7,15},{8,0},{9,1},... | collective-permute-start | bytes 387080 | tf_op jit(solution)/shard_map/ppermute | solution.py:238
  605.5 22.4 %collective-permute-start.11 = (bf16[1,56,1152]{2,1,0:T(8,128)(2,1)S(1)}, bf16[1,56,1152]{2,1,0:T(8,128)(2,1)S(1)}, u32[]{:S(2)}, u32[]{:S(2)}) collective-permute-start(bf16[1,56,1152]{2,1,0:T(8,128)(2,1)S(1)} %get-tuple-element.84), channel_id=1, source_target_pairs={{0,8},{1,9},{2,10},{3,11},{4,12},{5,13},{6,14},{7,15},{8,0},{9,1},... | collective-permute-start | bytes 387080 | tf_op jit(solution)/shard_map/ppermute | solution.py:238
  608.5 21.1 %collective-permute-start.4 = (bf16[1,56,1152]{2,1,0:T(8,128)(2,1)S(1)}, bf16[1,56,1152]{2,1,0:T(8,128)(2,1)S(1)}, u32[]{:S(2)}, u32[]{:S(2)}) collective-permute-start(bf16[1,56,1152]{2,1,0:T(8,128)(2,1)S(1)} %get-tuple-element.96), channel_id=1, source_target_pairs={{0,2},{1,3},{2,0},{3,1},{4,6},{5,7},{6,4},{7,5},{8,10},{9,11},{10,... | collective-permute-start | bytes 387080 | tf_op jit(solution)/shard_map/ppermute | solution.py:238
  629.6 17.9 %collective-permute-start.57 = (bf16[2,224,256]{2,1,0:T(8,128)(2,1)S(1)}, bf16[2,224,256]{2,1,0:T(8,128)(2,1)S(1)}, u32[]{:S(2)}, u32[]{:S(2)}) collective-permute-start(bf16[2,224,256]{2,1,0:T(8,128)(2,1)S(1)} %pad_maximum_fusion.31), channel_id=1, source_target_pairs={{0,8},{1,9},{2,10},{3,11},{4,12},{5,13},{6,14},{7,15},{8,0},{9,1},... | collective-permute-start | bytes 688136 | tf_op jit(solution)/shard_map/ppermute | solution.py:238
  632.3 22.3 %collective-permute-start.38 = (bf16[2,56,1152]{2,1,0:T(8,128)(2,1)S(1)}, bf16[2,56,1152]{2,1,0:T(8,128)(2,1)S(1)}, u32[]{:S(2)}, u32[]{:S(2)}) collective-permute-start(bf16[2,56,1152]{2,1,0:T(8,128)(2,1)S(1)} %pad_maximum_fusion.30), channel_id=1, source_target_pairs={{0,8},{1,9},{2,10},{3,11},{4,12},{5,13},{6,14},{7,15},{8,0},{9,1},... | collective-permute-start | bytes 774152 | tf_op jit(solution)/shard_map/ppermute | solution.py:238
  635.7 19.1 %collective-permute-start.31 = (bf16[2,56,1152]{2,1,0:T(8,128)(2,1)S(1)}, bf16[2,56,1152]{2,1,0:T(8,128)(2,1)S(1)}, u32[]{:S(2)}, u32[]{:S(2)}) collective-permute-start(bf16[2,56,1152]{2,1,0:T(8,128)(2,1)S(1)} %pad_maximum_fusion.29), channel_id=1, source_target_pairs={{0,2},{1,3},{2,0},{3,1},{4,6},{5,7},{6,4},{7,5},{8,10},{9,11},{10,... | collective-permute-start | bytes 774152 | tf_op jit(solution)/shard_map/ppermute | solution.py:238
  637.7 19.1 %collective-permute-start.12 = (bf16[2,56,1152]{2,1,0:T(8,128)(2,1)S(1)}, bf16[2,56,1152]{2,1,0:T(8,128)(2,1)S(1)}, u32[]{:S(2)}, u32[]{:S(2)}) collective-permute-start(bf16[2,56,1152]{2,1,0:T(8,128)(2,1)S(1)} %pad_maximum_fusion.28), channel_id=1, source_target_pairs={{0,2},{1,3},{2,0},{3,1},{4,6},{5,7},{6,4},{7,5},{8,10},{9,11},{10,... | collective-permute-start | bytes 774152 | tf_op jit(solution)/shard_map/ppermute | solution.py:238
  657.1 25.9 %collective-permute-start.58 = (bf16[4,224,256]{2,1,0:T(8,128)(2,1)S(1)}, bf16[4,224,256]{2,1,0:T(8,128)(2,1)S(1)}, u32[]{:S(2)}, u32[]{:S(2)}) collective-permute-start(bf16[4,224,256]{2,1,0:T(8,128)(2,1)S(1)} %pad_maximum_fusion.22), channel_id=1, source_target_pairs={{0,2},{1,3},{2,0},{3,1},{4,6},{5,7},{6,4},{7,5},{8,10},{9,11},{10,... | collective-permute-start | bytes 1376264 | tf_op jit(solution)/shard_map/ppermute | solution.py:238
  663.1 20.3 %collective-permute-start.39 = (bf16[4,56,1152]{2,1,0:T(8,128)(2,1)S(1)}, bf16[4,56,1152]{2,1,0:T(8,128)(2,1)S(1)}, u32[]{:S(2)}, u32[]{:S(2)}) collective-permute-start(bf16[4,56,1152]{2,1,0:T(8,128)(2,1)S(1)} %pad_maximum_fusion.21), channel_id=1, source_target_pairs={{0,2},{1,3},{2,0},{3,1},{4,6},{5,7},{6,4},{7,5},{8,10},{9,11},{10,... | collective-permute-start | bytes 1548296 | tf_op jit(solution)/shard_map/ppermute | solution.py:238
  664.1 21.0 %collective-permute-start.32 = (bf16[4,56,1152]{2,1,0:T(8,128)(2,1)S(1)}, bf16[4,56,1152]{2,1,0:T(8,128)(2,1)S(1)}, u32[]{:S(2)}, u32[]{:S(2)}) collective-permute-start(bf16[4,56,1152]{2,1,0:T(8,128)(2,1)S(1)} %pad_maximum_fusion.20), channel_id=1, source_target_pairs={{0,4},{1,5},{2,6},{3,7},{4,0},{5,1},{6,2},{7,3},{8,12},{9,13},{10,... | collective-permute-start | bytes 1548296 | tf_op jit(solution)/shard_map/ppermute | solution.py:238
  697.5 34.2 %collective-permute-start.33 = (bf16[8,56,1152]{2,1,0:T(8,128)(2,1)}, bf16[8,56,1152]{2,1,0:T(8,128)(2,1)}, u32[]{:S(2)}, u32[]{:S(2)}) collective-permute-start(bf16[8,56,1152]{2,1,0:T(8,128)(2,1)} %pad_maximum_fusion.11.refs_0_), channel_id=1, source_target_pairs={{0,1},{1,0},{2,3},{3,2},{4,5},{5,4},{6,7},{7,6},{8,9},{9,8},{10,11... | collective-permute-start | bytes 3096584 | tf_op jit(solution)/shard_map/ppermute | solution.py:238
  702.5 29.2 %collective-permute-start.47 = (bf16[8,56,1280]{2,1,0:T(8,128)(2,1)}, bf16[8,56,1280]{2,1,0:T(8,128)(2,1)}, u32[]{:S(2)}, u32[]{:S(2)}) collective-permute-start(bf16[8,56,1280]{2,1,0:T(8,128)(2,1)} %pad_maximum_fusion.8.refs_4_), channel_id=1, source_target_pairs={{0,1},{1,0},{2,3},{3,2},{4,5},{5,4},{6,7},{7,6},{8,9},{9,8},{10,11... | collective-permute-start | bytes 3440648 | tf_op jit(solution)/shard_map/ppermute | solution.py:238
  702.9 34.9 %collective-permute-start.21 = (bf16[8,56,1280]{2,1,0:T(8,128)(2,1)S(1)}, bf16[8,56,1280]{2,1,0:T(8,128)(2,1)}, u32[]{:S(2)}, u32[]{:S(2)}) collective-permute-start(bf16[8,56,1280]{2,1,0:T(8,128)(2,1)S(1)} %pad_maximum_fusion.7.refs_4_), channel_id=1, source_target_pairs={{0,1},{1,0},{2,3},{3,2},{4,5},{5,4},{6,7},{7,6},{8,9},{9,8},{10,11... | collective-permute-start | bytes 3440648 | tf_op jit(solution)/shard_map/ppermute | solution.py:238
  704.3 33.5 %collective-permute-start.14 = (bf16[8,56,1152]{2,1,0:T(8,128)(2,1)}, bf16[8,56,1152]{2,1,0:T(8,128)(2,1)S(1)}, u32[]{:S(2)}, u32[]{:S(2)}) collective-permute-start(bf16[8,56,1152]{2,1,0:T(8,128)(2,1)} %pad_maximum_fusion.10.refs_2_), channel_id=1, source_target_pairs={{0,1},{1,0},{2,3},{3,2},{4,5},{5,4},{6,7},{7,6},{8,9},{9,8},{10,11... | collective-permute-start | bytes 3096584 | tf_op jit(solution)/shard_map/ppermute | solution.py:238
  704.8 33.0 %collective-permute-start.7 = (bf16[8,56,1152]{2,1,0:T(8,128)(2,1)}, bf16[8,56,1152]{2,1,0:T(8,128)(2,1)S(1)}, u32[]{:S(2)}, u32[]{:S(2)}) collective-permute-start(bf16[8,56,1152]{2,1,0:T(8,128)(2,1)} %pad_maximum_fusion.9.refs_0_), channel_id=1, source_target_pairs={{0,1},{1,0},{2,3},{3,2},{4,5},{5,4},{6,7},{7,6},{8,9},{9,8},{10,11... | collective-permute-start | bytes 3096584 | tf_op jit(solution)/shard_map/ppermute | solution.py:238
  (95 other events, 1512.2 us)
Sparse Core Ops, SparseCore 0:
  370.0 58.9 all-gather.7
  467.3 60.5 all-gather.5
  594.6 58.0 all-gather.3
where the time goes:
time: 763 us; the launch traced here: 752 us
  Pallas kernels  373 us (49%)
  waiting for transfers between devices  180 us (24%)
  other arithmetic  93.5 us (12%)
  starting transfers between devices  77 us (10%)
  between operations  15 us (2%)
  local copies, waits for them, and re-layouts  13 us (2%)
    ppermute x78, waiting for transfers between devices, swap(): return lax.ppermute(t, 'dp', [(i, i ^ bit) for i in range(16)])  180 us
    ppermute x78, starting transfers between devices, swap(): return lax.ppermute(t, 'dp', [(i, i ^ bit) for i in range(16)])  76.5 us
    pallas_call x4, Pallas kernels, by_columns(): call(kernel, (ff // tile,), [pl.BlockSpec((t, d), lambda j, me: (0, 0)),...  76.2 us
    pallas_call x1, Pallas kernels, turn(): call(kernel, (ff // tile,), [whole, whole, w, w, pl.BlockSpec((None, tile...  54.5 us
    pallas_call x2, Pallas kernels, through(): call(kernel, (steps,), [wide, wide, w, w, o, o, *[pl.BlockSpec(memory_spa...  52.8 us
    convert_element_type x35, other arithmetic, add(): return functools.reduce(jnp.add, [t.astype(F32) for t in terms]).astype(BF)  50.5 us
    pallas_call x2, Pallas kernels, backward(): call(kernel, (steps,), [pl.BlockSpec((t, d), lambda j: (0, 0)), pl.BlockS...  48.2 us
    pallas_call x2, Pallas kernels, by_rows(): call(kernel, (4,), [pl.BlockSpec((t, ff // 4), lambda i, me: (0, i)), pl....  42.9 us
  transfers between devices with their start and end apart: 81, of which 24 were waited for; matrix products, arithmetic and copies ran while one was open for 13% of the time, Pallas kernels for 30%

commit v1 on v0

v1 whole, which is shorter than its diff:
```python
import jax
import jax.numpy as jnp
from jax import lax
from jax.experimental import pallas as pl
from jax.experimental.pallas import tpu as pltpu
from jax.sharding import PartitionSpec as P

BF, F32 = jnp.bfloat16, jnp.float32
CORE = 1
BIT = {"x": 8, "y": 4, "z": 2}
VMEM = 60 * 2**20


def dot(a, b, ca, cb):
    return lax.dot_general(a, b, (((ca,), (cb,)), ((), ())), preferred_element_type=F32)


def call(kernel, grid, ins, outs, shapes, flops, scratch=(), aliases={}, sums=(), collective_id=None):
    several = isinstance(shapes, list)
    outs, shapes = (outs, shapes) if several else ([outs], [shapes])
    n_in, n_out, n_scratch = len(ins), len(outs), len(scratch)
    hbm = pl.BlockSpec(memory_space=pl.ANY)
    sides, specs, extra, more = [], [], [], []
    for pieces, keep, send, _ in sums:
        rows, width = keep.shape[1:]
        sides += [keep, send]
        specs.append(pl.BlockSpec((rows, width), lambda i: (0, 0)))
        extra.append(jax.ShapeDtypeStruct((rows, width), BF))
        more.append(Side.scratch(pieces, rows))

    def whole(*refs):
        take = iter(refs)
        mine = [[next(take) for _ in range(n)] for n in (n_in, 2 * len(sums), n_out, len(sums), n_scratch)]
        running = [
            Side(one[0], mine[1][2 * k : 2 * k + 2], mine[3][k], [next(take) for _ in more[k]])
            for k, one in enumerate(sums)
        ]
        step = pl.program_id(0)
        for at in sorted({at for one in sums for at in one[3]}):

            @pl.when(step == at)
            def _():
                if at == 0:
                    greet()
                for side, one in zip(running, sums, strict=True):
                    for part, when in enumerate(one[3]):
                        if when == at:
                            side.run(part)

        kernel(*mine[0], *mine[2], *mine[4])
        if sums:

            @pl.when(step == grid[0] - 1)
            def _():
                for side in running:
                    side.end()

    out = pl.pallas_call(
        whole,
        grid=grid,
        in_specs=[*ins, *[hbm] * len(sides)],
        out_specs=[*outs, *specs],
        out_shape=[*shapes, *extra],
        scratch_shapes=[*scratch, *[one for group in more for one in group]],
        input_output_aliases=aliases,
        cost_estimate=pl.CostEstimate(flops=flops, bytes_accessed=flops // 400, transcendentals=0),
        compiler_params=pltpu.CompilerParams(
            vmem_limit_bytes=VMEM,
            dimension_semantics=("arbitrary",) * len(grid),
            collective_id=collective_id,
            has_side_effects=bool(sums),
        ),
    )

    def run(*args):
        got = out(*args, *sides)
        return got if several or sums else got[0]

    return run


def like(*shapes):
    return [jax.ShapeDtypeStruct(s, d) for s, d in shapes]


def scale_of(wide):
    return lax.rsqrt(jnp.mean(wide**2, -1, keepdims=True) + 1e-6)


def normed(h):
    wide = h.astype(F32)
    return (wide * scale_of(wide)).astype(BF)


def forward(a, w_gate, w_up, n, tile=512):
    t, d = a.shape
    ff = w_gate.shape[2]

    def kernel(a, wg, wu, gate, up, hid):
        g = dot(a[...], wg[...], 1, 0)
        u = dot(a[...], wu[...], 1, 0)
        gate[...] = g
        up[...] = u
        hid[...] = (g * sigmoid(g) * u).astype(BF)

    w = pl.BlockSpec((None, d, tile), lambda j: (n, 0, j))
    o = pl.BlockSpec((t, tile), lambda j: (0, j))
    return call(
        kernel,
        (ff // tile,),
        [pl.BlockSpec((t, d), lambda j: (0, 0)), w, w],
        [o, o, o],
        like(((t, ff), F32), ((t, ff), F32), ((t, ff), BF)),
        4 * t * d * ff,
    )(a, w_gate, w_up)


def down(x, hid, w_down, n, tile=512):
    t, d = x.shape
    ff = hid.shape[1]

    def kernel(x, hid, w, h, a):
        new = x[...].astype(F32) + dot(hid[...], w[...], 1, 0).astype(BF).astype(F32)
        new = new.astype(BF)
        h[...] = new
        a[...] = normed(new)

    o = pl.BlockSpec((tile, d), lambda i: (i, 0))
    return call(
        kernel,
        (t // tile,),
        [o, pl.BlockSpec((tile, ff), lambda i: (i, 0)), pl.BlockSpec((None, ff, d), lambda i: (n, 0, 0))],
        [o, o],
        like(((t, d), BF), ((t, d), BF)),
        2 * t * d * ff,
    )(x, hid, w_down)


def sigmoid(x):
    return 0.5 * jnp.tanh(0.5 * x) + 0.5


def gated_back(g, u, d_hid):
    d_hid = d_hid.astype(BF).astype(F32)
    s = sigmoid(g)
    act = g * s
    d_up = (d_hid * act).astype(BF)
    d_gate = (d_hid * u * (s + act * (1 - s))).astype(BF)
    return act, d_gate, d_up


def turn(a, back, w_gate, w_up, w_down, n, tile=256):
    t, d = a.shape
    ff = w_gate.shape[2]

    def kernel(a, back, wg, wu, wd, hid, d_gate, d_up):
        for r in range(0, t, 512):
            r = slice(r, r + 512)
            g = dot(a[r], wg[...], 1, 0)
            u = dot(a[r], wu[...], 1, 0)
            act, d_gate[r], d_up[r] = gated_back(g, u, dot(back[r], wd[...], 1, 1))
            hid[r] = (act * u).astype(BF)

    whole = pl.BlockSpec((t, d), lambda j: (0, 0))
    w = pl.BlockSpec((None, d, tile), lambda j: (n, 0, j))
    o = pl.BlockSpec((t, tile), lambda j: (0, j))
    return call(
        kernel,
        (ff // tile,),
        [whole, whole, w, w, pl.BlockSpec((None, tile, d), lambda j: (n, j, 0))],
        [o, o, o],
        like(*[((t, ff), BF)] * 3),
        6 * t * d * ff,
    )(a, back, w_gate, w_up, w_down)


def backward(back, gate, up, w_down, n, tile=512, sums=(), collective_id=None):
    t, d = back.shape
    ff = gate.shape[1]

    def kernel(back, wd, g, u, d_gate, d_up):
        for r in range(0, t, 512):
            r = slice(r, r + 512)
            _, d_gate[r], d_up[r] = gated_back(g[r], u[r], dot(back[r], wd[...], 1, 1))

    o = pl.BlockSpec((t, tile), lambda j: (0, j))
    return call(
        kernel,
        (ff // tile,),
        [once((t, d), lambda j: (0, 0)), pl.BlockSpec((None, tile, d), lambda j: (n, j, 0)), o, o],
        [o, o],
        like(*[((t, ff), BF)] * 2),
        2 * t * d * ff,
        sums=sums,
        collective_id=collective_id,
    )(back, w_down, gate, up)


def through(d_gate, d_up, w_gate, w_up, h, back, n, tile=256, sums=(), collective_id=None):
    t, d = h.shape
    ff = d_gate.shape[1]

    def kernel(dg, du, wg, wu, h, back, out):
        d_a = dot(dg[...], wg[...], 1, 1).astype(BF).astype(F32) + dot(du[...], wu[...], 1, 1).astype(BF).astype(F32)
        d_a = d_a.astype(BF).astype(F32)
        wide = h[...].astype(F32)
        scale = scale_of(wide)
        along = jnp.mean(d_a * wide, -1, keepdims=True)
        d_h = scale * d_a - wide * (scale**3 * along)
        out[...] = (back[...].astype(F32) + d_h.astype(BF).astype(F32)).astype(BF)

    o = pl.BlockSpec((tile, d), lambda i: (i, 0))
    wide = pl.BlockSpec((tile, ff), lambda i: (i, 0))
    w = once((None, d, ff), lambda i: (n, 0, 0))
    return call(
        kernel,
        (t // tile,),
        [wide, wide, w, w, o, o],
        o,
        like(((t, d), BF))[0],
        4 * t * d * ff,
        sums=sums,
        collective_id=collective_id,
    )(d_gate, d_up, w_gate, w_up, h, back)


def once(shape, index):
    return pl.BlockSpec(shape, index, pipeline_mode=pl.Buffered(1))


def by_columns(a, bs, tile=512, sums=(), collective_id=None):
    t, d = a.shape
    ff = bs[0].shape[1]
    rows, steps = d // 16, ff // tile

    def kernel(a, *refs):
        ins, outs, acc = refs[: len(bs)], refs[len(bs) : -1], refs[-1]
        me = lax.axis_index("dp")
        for k in range(len(bs)):

            @pl.when(pl.program_id(0) // steps == k)
            def _():
                acc[...] = dot(a[...], ins[k][...], 0, 0).reshape(acc.shape)
                for j in range(8):
                    outs[2 * k][j] = acc[(2 * j) ^ me].astype(BF)
                    outs[2 * k + 1][j] = acc[(2 * j + 1) ^ me].astype(BF)

    def at(k):
        return lambda i: jnp.clip(i - k * steps, 0, steps - 1)

    ins = [pl.BlockSpec((t, tile), lambda i, k=k: (0, at(k)(i))) for k in range(len(bs))]
    outs = [pl.BlockSpec((8, rows, tile), lambda i, k=k: (0, 0, at(k)(i))) for k in range(len(bs)) for _ in range(2)]
    return call(
        kernel,
        (steps * len(bs),),
        [once((t, d), lambda i: (0, 0)), *ins],
        outs,
        like(*[((8, rows, ff), BF)] * (2 * len(bs))),
        2 * t * d * ff * len(bs),
        scratch=[pltpu.VMEM((16, rows, tile), F32)],
        sums=sums,
        collective_id=collective_id,
    )(a, *bs)


def by_rows(a, b):
    t, ff = a.shape
    d = b.shape[1]
    rows = ff // 16

    def kernel(a, b, keep, send, acc):
        acc[...] = dot(a[...], b[...], 0, 0).reshape(acc.shape)
        low = lax.axis_index("dp") & 3
        for j in range(2):
            keep[j] = acc[(2 * j) ^ low].astype(BF)
            send[j] = acc[(2 * j + 1) ^ low].astype(BF)

    o = pl.BlockSpec((2, rows, d), lambda i: (i ^ (lax.axis_index("dp") >> 2), 0, 0))
    return call(
        kernel,
        (4,),
        [pl.BlockSpec((t, ff // 4), lambda i: (0, i)), once((t, d), lambda i: (0, 0))],
        [o, o],
        like(*[((8, rows, d), BF)] * 2),
        2 * t * d * ff,
        scratch=[pltpu.VMEM((4, rows, d), F32)],
    )(a, b)


def put(full, n, layers, onto):
    rows, width = full.shape[0] // 16, full.shape[1]

    def kernel(full, *refs):
        refs[-1][...] = full[...]

    more = [] if onto is None else [onto]
    return call(
        kernel,
        (4,),
        [pl.BlockSpec((2, 2, rows, width), lambda k: (k, 0, 0, 0)), *[pl.BlockSpec(memory_space=pl.ANY) for _ in more]],
        pl.BlockSpec((None, 2, 2, rows, width), lambda k: (n, k, 0, 0, 0)),
        like(((layers, 8, 2, rows, width), BF))[0],
        10**9,
        aliases={1: 0} if more else {},
    )(full.reshape(8, 2, rows, width), *more)


def placed(parts, pieces, n, onto):
    _, _, _, rows, width = onto.shape

    def kernel(*refs):
        out, held, came, went = refs[-4:]
        me = lax.axis_index("dp")
        core, pair = me & 1, me >> 1

        def copies(j):
            bits = {"x": j >> 2, "y": (j >> 1) & 1, "z": j & 1}
            k = pair ^ j
            for i, (start, stop, order) in enumerate(pieces):
                at = bits[order[0]] * 4 + bits[order[1]] * 2 + bits[order[2]]
                for side in range(2):
                    yield pltpu.make_async_copy(
                        refs[i].at[8 * side + at],
                        held.at[k, core ^ side, :, start:stop],
                        came.at[j, 2 * i + side],
                    )

        def leave(j):
            k = pair ^ j
            return pltpu.make_async_copy(held.at[k], out.at[n, k], went.at[j])

        for j in range(8):
            for copy in copies(j):
                copy.start()
        for j in range(8):
            for copy in copies(j):
                copy.wait()
            leave(j).start()
        for j in range(8):
            leave(j).wait()

    whole = pl.BlockSpec(memory_space=pl.ANY)
    return pl.pallas_call(
        kernel,
        in_specs=[whole] * (len(parts) + 1),
        out_specs=whole,
        out_shape=jax.ShapeDtypeStruct(onto.shape, BF),
        input_output_aliases={len(parts): 0},
        scratch_shapes=[
            pltpu.VMEM((8, 2, rows, width), BF),
            pltpu.SemaphoreType.DMA((8, 2 * len(parts))),
            pltpu.SemaphoreType.DMA((8,)),
        ],
        cost_estimate=pl.CostEstimate(flops=10**9, bytes_accessed=10**7, transcendentals=0),
        compiler_params=pltpu.CompilerParams(vmem_limit_bytes=VMEM),
        name="placed",
    )(*parts, onto)


BITS = {"x": 4, "y": 2, "z": 1}


def peer(bit):
    return {"dp": lax.axis_index("dp") ^ bit}


def remote(src, dst, sems, i, bit):
    return pltpu.make_async_remote_copy(
        src, dst, sems[0].at[i], sems[1].at[i], device_id=peer(bit), device_id_type=pl.DeviceIdType.MESH
    )


def greet():
    barrier = pltpu.get_barrier_semaphore()
    for bit in (CORE, *BIT.values()):
        pl.semaphore_signal(barrier, inc=1, device_id=peer(bit), device_id_type=pl.DeviceIdType.MESH)
    pl.semaphore_wait(barrier, 4)


class Summed:
    def __init__(self, pieces, refs):
        self.pieces = pieces
        self.mine, self.other = refs[:2]
        self.out = [refs[2 + 3 * i : 5 + 3 * i] for i in range(3)]
        self.got = [refs[11 + 3 * i : 14 + 3 * i] for i in range(3)]
        self.sems = refs[20:22]

    @staticmethod
    def scratch(pieces, rows):
        width = pieces[-1][1]
        whole = [pltpu.VMEM((8, rows, width), BF)] * 2
        halves = [pltpu.VMEM((n, rows, stop - start), BF) for start, stop, _ in pieces for n in (4, 2, 1)]
        return [*whole, *halves, *halves, pltpu.SemaphoreType.DMA((9,)), pltpu.SemaphoreType.DMA((9,))]

    def copy(self, i, stage):
        return remote(self.out[i][stage], self.got[i][stage], self.sems, 3 * i + stage, BIT[self.pieces[i][2][stage]])

    def term(self, i, stage, j):
        start, stop, order = self.pieces[i]
        total = self.mine[j, :, start:stop].astype(F32) + self.other[j, :, start:stop].astype(F32)
        for past in range(stage):
            total = total + self.got[i][past][self.place(order, past, j)].astype(F32)
        return total

    @staticmethod
    def place(order, stage, j):
        rest = [axis for axis in "xyz" if axis not in order[: stage + 1]]
        return sum(bool(j & BITS[axis]) << (len(rest) - 1 - k) for k, axis in enumerate(rest))

    def send(self, stage):
        for i, (_, _, order) in enumerate(self.pieces):
            if stage:
                self.copy(i, stage - 1).wait_recv()
            for j in range(8):
                gone = any(j & BITS[axis] for axis in order[:stage])
                if j & BITS[order[stage]] and not gone:
                    self.out[i][stage][self.place(order, stage, j)] = self.term(i, stage, j).astype(BF)
            self.copy(i, stage).start()

    def total(self, i):
        self.copy(i, 2).wait_recv()
        return self.term(i, 3, 0).astype(BF).astype(F32)

    def finish(self):
        for i in range(3):
            for stage in range(3):
                self.copy(i, stage).wait_send()


class Side:
    def __init__(self, pieces, ins, out, refs):
        self.pieces, self.keep, self.send, self.out = pieces, *ins, out
        self.sum, self.core, self.load = Summed(pieces, refs[:22]), refs[22:24], refs[24]

    @staticmethod
    def scratch(pieces, rows):
        return [*Summed.scratch(pieces, rows), *[pltpu.SemaphoreType.DMA((1,))] * 3]

    def copies(self):
        return (
            pltpu.make_async_copy(self.keep, self.sum.mine, self.load.at[0]),
            remote(self.send, self.sum.other, self.core, 0, CORE),
        )

    def run(self, part):
        if part == 0:
            for copy in self.copies():
                copy.start()
            return
        if part == 1:
            for copy in self.copies():
                copy.wait()
        self.sum.send(part - 1)

    def end(self):
        for i, (start, stop, _) in enumerate(self.pieces):
            self.out[:, start:stop] = self.sum.total(i).astype(BF)
        self.sum.finish()


class Spread:
    def __init__(self, pieces, own, outs, sems):
        self.pieces, self.own, self.outs = pieces, own, outs
        self.sems, self.local = sems[:2], sems[2]

    @staticmethod
    def scratch():
        return [pltpu.SemaphoreType.DMA((21,)), pltpu.SemaphoreType.DMA((21,)), pltpu.SemaphoreType.DMA((3,))]

    def along(self, i, stage):
        n = 1 << stage
        out = self.outs[i]
        src = out.at[pl.ds(0, n)] if stage else self.own[i]
        dst = out.at[pl.ds(n, n)] if stage else out.at[1]
        return remote(src, dst, self.sems, 7 * i + stage, BIT[self.pieces[i][2][2 - stage]])

    def across(self, i, stage):
        out = self.outs[i]
        n = 1 << (stage - 1) if stage else 1
        src = out.at[pl.ds(n, n)] if stage else self.own[i]
        dst = out.at[pl.ds(8 + n, n)] if stage else out.at[8]
        return remote(src, dst, self.sems, 7 * i + 3 + stage, CORE)

    def keep(self, i):
        return pltpu.make_async_copy(self.own[i], self.outs[i].at[0], self.local.at[i])

    def begin(self, i):
        self.along(i, 0).start()
        self.keep(i).start()
        self.across(i, 0).start()

    def step(self, stage):
        for i in range(3):
            self.along(i, stage).wait_recv()
            if stage == 0:
                self.keep(i).wait()
            if stage < 2:
                self.along(i, stage + 1).start()
            self.across(i, stage + 1).start()

    def finish(self):
        for i in range(3):
            for stage in range(3):
                self.along(i, stage).wait_send()
            for stage in range(4):
                self.across(i, stage).wait()


def tail(gate, up, states, pieces):
    rows, width = gate[0].shape[1:]

    def kernel(*refs):
        w_in, m_in, v_in = ((refs[4 + k], refs[7 + k]) for k in range(3))
        outs = [refs[10 + 3 * k : 13 + 3 * k] for k in range(2)]
        m_out, v_out = refs[16:18], refs[18:20]
        sides = [Side(pieces[k], refs[2 * k : 2 * k + 2], None, refs[20 + 25 * k : 45 + 25 * k]) for k in range(2)]
        own = [refs[70:73], refs[73:76]]
        spread = [Spread(pieces[k], own[k], outs[k], refs[76 + 3 * k : 79 + 3 * k]) for k in range(2)]
        greet()
        for part in range(4):
            for side in sides:
                side.run(part)
        for k in range(2):
            for i, (start, stop, _) in enumerate(pieces[k]):
                cols = slice(start, stop)
                new, m_out[k][:, cols], v_out[k][:, cols] = adamw(
                    w_in[k][:, cols].astype(F32), m_in[k][:, cols], v_in[k][:, cols], sides[k].sum.total(i)
                )
                own[k][i][...] = new
                spread[k].begin(i)
        for stage in range(3):
            for k in range(2):
                spread[k].step(stage)
        for k in range(2):
            sides[k].sum.finish()
            spread[k].finish()

    hbm, vmem = pl.BlockSpec(memory_space=pl.ANY), pl.BlockSpec(memory_space=pltpu.VMEM)
    arrays = [jax.ShapeDtypeStruct((16, rows, stop - start), BF) for k in range(2) for start, stop, _ in pieces[k]]
    state = [jax.ShapeDtypeStruct((rows, width), F32)] * 4
    out = pl.pallas_call(
        kernel,
        in_specs=[hbm] * 4 + [vmem] * 6,
        out_specs=[hbm] * 6 + [vmem] * 4,
        out_shape=[*arrays, *state],
        scratch_shapes=[
            *Side.scratch(pieces[0], rows),
            *Side.scratch(pieces[1], rows),
            *[pltpu.VMEM((rows, stop - start), BF) for k in range(2) for start, stop, _ in pieces[k]],
            *Spread.scratch() * 2,
        ],
        cost_estimate=pl.CostEstimate(flops=10**11, bytes_accessed=10**8, transcendentals=0),
        compiler_params=pltpu.CompilerParams(collective_id=1, has_side_effects=True, vmem_limit_bytes=VMEM),
        name="tail",
    )(*gate, *up, *states[0], *states[1])
    return [out[3 * k : 3 * k + 3] for k in range(2)], out[6:8], out[8:10]


def adamw(w, m, v, g):
    m = 0.9 * m + 0.1 * g
    v = 0.95 * v + 0.05 * g * g
    step = m * lax.rsqrt(v + 1e-8) + 0.1 * w
    return (w - 0.02 * step).astype(BF), m, v


def solution(mesh):
    ORDERS = ("xyz", "yzx", "zxy")

    def body(x, dy, w_gate, w_up, w_down, *moments):
        x, dy = x[0], dy[0]
        m, v = moments[:3], moments[3:]
        me = lax.axis_index("dp")
        weights = (w_gate, w_up, w_down)
        new = [[None] * 2 for _ in range(9)]
        whole = [None] * 3

        def pieces_of(which):
            cuts = [0, 256, 512, 896] if which == 2 else [0, 1152, 2304, 3584]
            return [(cuts[i], cuts[i + 1], ORDERS[(which + i) % 3]) for i in range(3)]

        def state(which, n):
            rows, width = weights[which].shape[1] // 16, weights[which].shape[2]
            w = lax.dynamic_slice(weights[which], (n, me * rows, 0), (1, rows, width))[0]
            return w, m[which][n], v[which][n]

        def update(which, n, g):
            w, m1, v1 = state(which, n)
            w, new[3 + which][n], new[6 + which][n] = adamw(w.astype(F32), m1, v1, g.astype(F32))
            whole[which] = put(lax.all_gather(w, "dp", axis=0, tiled=True), n, 2, whole[which])

        a0 = normed(x)
        gate, up, hid0 = forward(a0, w_gate, w_up, 0)
        h, a1 = down(x, hid0, w_down, 0)
        hid1, d_gate, d_up = turn(a1, dy, w_gate, w_up, w_down, 1)
        down1 = by_rows(hid1, dy)
        *both, g = by_columns(a1, (d_gate, d_up), sums=[(pieces_of(2), *down1, (0, 3, 8, 11))], collective_id=2)
        update(2, 1, g)
        sums = [(pieces_of(0), *both[:2], (0, 2, 4, 6)), (pieces_of(1), *both[2:], (0, 3, 5, 7))]
        back, *g = through(d_gate, d_up, w_gate, w_up, h, dy, 1, sums=sums, collective_id=3)
        update(0, 1, g[0])
        update(1, 1, g[1])
        sums = [(pieces_of(2), *by_rows(hid0, back), (0, 2, 4, 5))]
        d_gate, d_up, g = backward(back, gate, up, w_down, 0, sums=sums, collective_id=4)
        update(2, 0, g)
        both = by_columns(a0, (d_gate, d_up))
        pieces = [pieces_of(which) for which in range(2)]
        parts, ms, vs = tail(both[:2], both[2:], (state(0, 0), state(1, 0)), pieces)
        for which in range(2):
            new[3 + which][0], new[6 + which][0] = ms[which], vs[which]
            whole[which] = placed(parts[which], pieces[which], 0, whole[which])
        for i in range(3):
            new[i] = whole[i].reshape(weights[i].shape)
        return tuple(one if i < 3 else jnp.stack(one) for i, one in enumerate(new))

    seq = P(("rep", "dp"), None, None)
    full = P(None, None, None)
    block = P(None, "dp", None)
    return jax.shard_map(
        body,
        mesh=mesh,
        in_specs=(seq, seq, *[full] * 3, *[block] * 6),
        out_specs=(*[P("rep", None, None)] * 3, *[P("rep", "dp", None)] * 6),
        check_vma=False,
    )
```

time: 763 us -> 579 us (0.76)
  waiting for transfers between devices: 180 us -> 1.26 us
  Pallas kernels: 373 us -> 524 us
  starting transfers between devices: 77 us -> 0.16 us
  other arithmetic: 93.5 us -> 22.1 us
    ppermute x78 -> x0, waiting for transfers between devices: 180 us -> none  [swap(): return lax.ppermute(t, 'dp', [(i, i ^ bit) for i in range(16)])]
    pallas_call x19 -> x16, Pallas kernels: 373 us -> 524 us  [the longest x13 393 us: run(): got = out(*args, *sides)]
    ppermute x78 -> x0, starting transfers between devices: 76.5 us -> none  [swap(): return lax.ppermute(t, 'dp', [(i, i ^ bit) for i in range(16)])]
    convert_element_type x35 -> x1, other arithmetic: 50.5 us -> 4.14 us  [adamw(): return ((w - 0.02 * step).astype(BF), m, v)]
    another operation x15 -> x6, other arithmetic: 22.2 us -> 12.5 us  [body(): jnp.stack(one)]
    broadcast_in_dim x6 -> x0, other arithmetic: 9.4 us -> none  [gathered(): held = block[None]]
  transfers between devices with their start and end apart: 81 -> 4, of which waited for: 24 -> 0; matrix products, arithmetic and copies ran while one was open for 13% -> 4% of each run, Pallas kernels for 30% -> 45%
where the time goes in v1:
time: 579 us; the launch traced here: 570 us
  Pallas kernels  524 us (91%)
  other arithmetic  22.1 us (4%)
  between operations  14.2 us (2%)
  local copies, waits for them, and re-layouts  7.83 us (1%)
    pallas_call x13, Pallas kernels, run(): got = out(*args, *sides)  393 us
    pallas_call x1, Pallas kernels, tail(): pl.pallas_call(kernel, in_specs=[hbm] * 4 + [vmem] * 6, out_specs=[hbm] *...  119 us
    another operation x6, other arithmetic, body(): jnp.stack(one)  12.5 us
    pallas_call x2, Pallas kernels, placed(): pl.pallas_call(kernel, in_specs=[whole] * (len(parts) + 1), out_specs=who...  12.1 us
  transfers between devices with their start and end apart: 4, of which 0 were waited for; matrix products, arithmetic and copies ran while one was open for 4% of the time, Pallas kernels for 45%

profile of v1, /device:TPU:0, one launch (start us, length us, event | category | flops | bytes accessed | tf_op | source)
XLA Modules:
  0.0 569.6 jit_solution(7071996251906035036)
XLA Ops:
  7.2 0.0 all-gather.5.cloned.1.call-start
  7.2 0.0 copy-start
  7.2 3.0 fusion
  10.2 0.1 copy-done
  10.4 2.5 fusion.1.refs_0_
  12.9 40.1 %shard_map.178 = (f32[2048,3584]{1,0:T(8,128)}, f32[2048,3584]{1,0:T(8,128)}, bf16[2048,3584]{1,0:T(8,128)(2,1)}) custom-call(bf16[2048,896]{1,0:T(8,128)(2,1)} %fusion.1.refs_0_, bf16[2,896,3584]{2,1,0:T(8,128)(2,1)} %refs_2_.7, bf16[2,896,3584]{2,1,0:T(8,128)(2,1)} %refs_3_.3), custom_call_target="tpu_custom_call" | custom-call | flops 26306674688 | bytes 65766688 | tf_op jit(solution)/shard_map/pallas_call | solution.py:76
  53.0 22.5 %shard_map.179 = (bf16[2048,896]{1,0:T(8,128)(2,1)}, bf16[2048,896]{1,0:T(8,128)(2,1)}) custom-call(bf16[2048,896]{1,0:T(8,128)(2,1)} %bitcast.106, bf16[2048,3584]{1,0:T(8,128)(2,1)} %get-tuple-element.46.refs_1_.refs_0_, bf16[2,3584,896]{2,1,0:T(8,128)(2,1)} %refs_1_.3), custom_call_target="tpu_custom_call" | custom-call | flops 13153337344 | bytes 32883344 | tf_op jit(solution)/shard_map/pallas_call | solution.py:76
  75.5 54.5 %shard_map.180 = (bf16[2048,3584]{1,0:T(8,128)(2,1)}, bf16[2048,3584]{1,0:T(8,128)(2,1)}, bf16[2048,3584]{1,0:T(8,128)(2,1)}) custom-call(bf16[2048,896]{1,0:T(8,128)(2,1)} %get-tuple-element.47.refs_0_, bf16[2048,896]{1,0:T(8,128)(2,1)} %bitcast.115, bf16[2,896,3584]{2,1,0:T(8,128)(2,1)} %refs_2_.7, bf16[2,896,3584]{2,1,0:T(8,128)(2,1)} %refs_3_.3, ...), custom_call_target="tpu_custom_call" | custom-call | flops 39460012032 | bytes 98650032 | tf_op jit(solution)/shard_map/pallas_call | solution.py:76
  130.0 21.4 %shard_map.181 = (bf16[8,224,896]{2,1,0:T(8,128)(2,1)}, bf16[8,224,896]{2,1,0:T(8,128)(2,1)}) custom-call(bf16[2048,3584]{1,0:T(8,128)(2,1)} %get-tuple-element.51.refs_0_, bf16[2048,896]{1,0:T(8,128)(2,1)} %bitcast.116), custom_call_target="tpu_custom_call" | custom-call | flops 13153337344 | bytes 32883344 | tf_op jit(solution)/shard_map/pallas_call | solution.py:76
  151.3 49.1 %shard_map.182 = (bf16[8,56,3584]{2,1,0:T(8,128)(2,1)}, bf16[8,56,3584]{2,1,0:T(8,128)(2,1)}, bf16[8,56,3584]{2,1,0:T(8,128)(2,1)}, bf16[8,56,3584]{2,1,0:T(8,128)(2,1)}, bf16[224,896]{1,0:T(8,128)(2,1)}) custom-call(bf16[2048,896]{1,0:T(8,128)(2,1)} %get-tuple-element.47.refs_0_, bf16[2048,3584]{1,0:T(8,128)(2,1)} %get-tuple-element.48.refs_1_.refs_0_, ...), custom_call_target="tpu_custom_call" | custom-call | flops 26306674688 | bytes 65766688 | tf_op jit(solution)/shard_map/pallas_call | solution.py:76
  200.4 0.0 copy-start.5
  200.4 0.0 copy-start.6
  200.4 60.5 %shard_map.183 = (bf16[2048,896]{1,0:T(8,128)(2,1)}, bf16[56,3584]{1,0:T(8,128)(2,1)}, bf16[56,3584]{1,0:T(8,128)(2,1)}) custom-call(bf16[2048,3584]{1,0:T(8,128)(2,1)} %get-tuple-element.48.refs_1_.refs_0_, bf16[2048,3584]{1,0:T(8,128)(2,1)} %get-tuple-element.49.refs_2_.refs_1_, bf16[2,896,3584]{2,1,0:T(8,128)(2,1)} %refs_2_.7, ...), custom_call_target="tpu_custom_call" | custom-call | flops 26306674688 | bytes 65766688 | tf_op jit(solution)/shard_map/pallas_call | solution.py:76
  261.0 0.0 copy-done.5
  261.0 0.0 copy-done.6
  261.0 4.2 fusion.28
  265.2 0.0 all-gather.5.cloned.1.call-update
  265.2 0.0 all-gather.7.cloned.1.call-start
  265.3 0.7 all-gather.7.cloned.1.call-update
  266.0 0.0 all-gather.11.cloned.1.call-start
  266.0 21.5 %shard_map.184 = (bf16[8,224,896]{2,1,0:T(8,128)(2,1)}, bf16[8,224,896]{2,1,0:T(8,128)(2,1)}) custom-call(bf16[2048,3584]{1,0:T(8,128)(2,1)} %get-tuple-element.46.refs_1_.refs_0_, bf16[2048,896]{1,0:T(8,128)(2,1)} %get-tuple-element.58.refs_1_.refs_0_), custom_call_target="tpu_custom_call" | custom-call | flops 13153337344 | bytes 32883344 | tf_op jit(solution)/shard_map/pallas_call | solution.py:76
  287.6 63.2 %shard_map.185 = (bf16[2048,3584]{1,0:T(8,128)(2,1)}, bf16[2048,3584]{1,0:T(8,128)(2,1)}, bf16[224,896]{1,0:T(8,128)(2,1)}) custom-call(bf16[2048,896]{1,0:T(8,128)(2,1)} %get-tuple-element.58.refs_1_.refs_0_, bf16[2,3584,896]{2,1,0:T(8,128)(2,1)} %refs_1_.3, f32[2048,3584]{1,0:T(8,128)} %get-tuple-element.59.refs_2_, ...), custom_call_target="tpu_custom_call" | custom-call | flops 13153337344 | bytes 32883344 | tf_op jit(solution)/shard_map/pallas_call | solution.py:76
  350.8 0.0 copy-done.12
  350.8 4.1 fusion.17
  354.9 0.0 all-gather.11.cloned.1.call-update
  354.9 0.0 all-gather.9.cloned.1.call-start
  355.0 0.5 all-gather.9.cloned.1.call-update
  355.5 0.0 copy-start.7
  355.5 0.0 copy-start.8
  355.5 1.9 dynamic-slice_bitcast_fusion.1.refs_4_
  357.5 2.6 slice_bitcast_fusion.2
  360.1 1.3 slice_bitcast_fusion
  361.4 36.3 %shard_map.186 = (bf16[8,56,3584]{2,1,0:T(8,128)(2,1)}, bf16[8,56,3584]{2,1,0:T(8,128)(2,1)}, bf16[8,56,3584]{2,1,0:T(8,128)(2,1)}, bf16[8,56,3584]{2,1,0:T(8,128)(2,1)}) custom-call(bf16[2048,896]{1,0:T(8,128)(2,1)} %fusion.1.refs_0_, bf16[2048,3584]{1,0:T(8,128)(2,1)} %get-tuple-element.63.refs_1_, bf16[2048,3584]{1,0:T(8,128)(2,1)} %get-tuple-element.64.refs_2_), custom_call_target="tpu_custom_call" | custom-call | flops 26306674688 | bytes 65766688 | tf_op jit(solution)/shard_map/pallas_call | solution.py:76
  397.8 1.9 pad_maximum_fusion.2
  399.7 1.8 dynamic-slice_bitcast_fusion.refs_7_
  401.4 118.8 %tail.1 = (bf16[16,56,1152]{2,1,0:T(8,128)(2,1)}, bf16[16,56,1152]{2,1,0:T(8,128)(2,1)}, bf16[16,56,1280]{2,1,0:T(8,128)(2,1)}, bf16[16,56,1152]{2,1,0:T(8,128)(...) custom-call(bf16[8,56,3584]{2,1,0:T(8,128)(2,1)} %get-tuple-element., ...), custom_call_target="tpu_custom_call" | custom-call | flops 99999997952 | bytes 100000000 | tf_op jit(solution)/shard_map/tail/pallas_call | solution.py:541
  520.3 2.6 pad_maximum_fusion
  522.9 1.3 pad_maximum_fusion.1
  524.1 0.0 copy-done.10
  524.2 1.3 pad_maximum_fusion.3
  525.4 0.0 copy-done.9
  525.4 1.3 pad_maximum_fusion.4
  526.7 6.0 %shard_map.187.refs_3_ = bf16[2,8,2,56,3584]{4,3,2,1,0:T(8,128)(2,1)} custom-call(bf16[8,2,56,3584]{3,2,1,0:T(8,128)(2,1)} %bitcast.107), custom_call_target="tpu_custom_call" | custom-call | flops 1000000000 | bytes 2500000 | tf_op jit(solution)/shard_map/pallas_call | solution.py:76
  532.7 6.0 %shard_map.188.refs_3_ = bf16[2,8,2,56,3584]{4,3,2,1,0:T(8,128)(2,1)} custom-call(bf16[8,2,56,3584]{3,2,1,0:T(8,128)(2,1)} %bitcast.108), custom_call_target="tpu_custom_call" | custom-call | flops 1000000000 | bytes 2500000 | tf_op jit(solution)/shard_map/pallas_call | solution.py:76
  538.7 6.0 %shard_map.189.refs_1_ = bf16[2,8,2,224,896]{4,3,2,1,0:T(8,128)(2,1)} custom-call(bf16[8,2,224,896]{3,2,1,0:T(8,128)(2,1)} %bitcast.109), custom_call_target="tpu_custom_call" | custom-call | flops 1000000000 | bytes 2500000 | tf_op jit(solution)/shard_map/pallas_call | solution.py:76
  544.7 6.0 %shard_map.190 = bf16[2,8,2,224,896]{4,3,2,1,0:T(8,128)(2,1)} custom-call(bf16[8,2,224,896]{3,2,1,0:T(8,128)(2,1)} %bitcast.110, bf16[2,8,2,224,896]{4,3,2,1,0:T(8,128)(2,1)} %shard_map.189.refs_1_), custom_call_target="tpu_custom_call", output_to_operand_aliasing={{}: (1, {})} | custom-call | flops 1000000000 | bytes 2500000 | tf_op jit(solution)/shard_map/pallas_call | solution.py:76
  550.7 6.0 %placed.2 = bf16[2,8,2,56,3584]{4,3,2,1,0:T(8,128)(2,1)} custom-call(bf16[16,56,1152]{2,1,0:T(8,128)(2,1)} %get-tuple-element.69.refs_0_, bf16[16,56,1152]{2,1,0:T(8,128)(2,1)} %get-tuple-element.70.refs_1_, bf16[16,56,1280]{2,1,0:T(8,128)(2,1)} %get-tuple-element.71.refs_2_, ...), custom_call_target="tpu_custom_call", output_to_operand_aliasing={{}: (3, {})} | custom-call | flops 1000000000 | bytes 10000000 | tf_op jit(solution)/shard_map/placed/pallas_call | solution.py:343
  556.7 6.0 %placed.3 = bf16[2,8,2,56,3584]{4,3,2,1,0:T(8,128)(2,1)} custom-call(bf16[16,56,1152]{2,1,0:T(8,128)(2,1)} %get-tuple-element.73.refs_0_, bf16[16,56,1152]{2,1,0:T(8,128)(2,1)} %get-tuple-element.74.refs_1_, bf16[16,56,1280]{2,1,0:T(8,128)(2,1)} %get-tuple-element.75.refs_2_, ...), custom_call_target="tpu_custom_call", output_to_operand_aliasing={{}: (3, {})} | custom-call | flops 1000000000 | bytes 10000000 | tf_op jit(solution)/shard_map/placed/pallas_call | solution.py:343
  (20 shorter events, 0.0 us)
Async XLA Ops:
  7.2 519.5 %all-gather.5.cloned.1.call-start = ((), (), s32[]{:S(2)}) async-start(), calls=%async_computation | async-start | bytes 6823936 | tf_op jit(solution)/shard_map/all_gather | solution.py:589
  7.2 3.1 copy-start
  200.4 60.6 %copy-start.5 = (f32[2,56,3584]{2,1,0:T(8,128)S(1)}, f32[2,56,3584]{2,1,0:T(8,128)}, u32[]{:S(2)}) copy-start(f32[2,56,3584]{2,1,0:T(8,128)} %param.19) | copy-start | bytes 4816900
  200.4 60.6 %copy-start.6 = (f32[2,56,3584]{2,1,0:T(8,128)S(1)}, f32[2,56,3584]{2,1,0:T(8,128)}, u32[]{:S(2)}) copy-start(f32[2,56,3584]{2,1,0:T(8,128)} %param.16) | copy-start | bytes 4816900
  265.2 267.4 %all-gather.7.cloned.1.call-start = ((), (), s32[]{:S(2)}) async-start(), calls=%async_computation.1 | async-start | bytes 6823936 | tf_op jit(solution)/shard_map/all_gather | solution.py:589
  266.0 272.7 %all-gather.11.cloned.1.call-start = ((), (), s32[]{:S(2)}) async-start(), calls=%async_computation.3 | async-start | bytes 6823936 | tf_op jit(solution)/shard_map/all_gather | solution.py:589
  287.6 63.2 %copy-start.12 = (bf16[224,896]{1,0:T(8,128)(2,1)S(1)}, bf16[224,896]{1,0:T(8,128)(2,1)}, u32[]{:S(2)}) copy-start(bf16[224,896]{1,0:T(8,128)(2,1)} %get-tuple-element.78) | copy-start | bytes 1204228
  354.9 189.7 %all-gather.9.cloned.1.call-start = ((), (), s32[]{:S(2)}) async-start(), calls=%async_computation.2 | async-start | bytes 6823936 | tf_op jit(solution)/shard_map/all_gather | solution.py:589
  355.5 4.6 copy-start.7
  355.5 4.6 copy-start.8
  401.4 118.9 %copy-start.4 = (f32[1,56,3584]{2,1,0:T(8,128)S(1)}, f32[1,56,3584]{2,1,0:T(8,128)}, u32[]{:S(2)}) copy-start(f32[1,56,3584]{2,1,0:T(8,128)} %get-tuple-element.95) | copy-start | bytes 2408452
  520.3 2.6 copy-start.3
  520.3 2.6 copy-start.11
  520.3 3.9 copy-start.2
  520.3 3.9 copy-start.10
  522.9 2.5 copy-start.1
  522.9 2.5 copy-start.9
Sparse Core Ops, SparseCore 0:
  265.4 42.1 all-gather.4
  309.8 50.8 all-gather.6
  362.9 42.5 all-gather.10
  407.7 62.9 all-gather.8

commit v2 on v1

v2 whole, which is shorter than its diff:
```python
import jax
import jax.numpy as jnp
from jax import lax
from jax.experimental import pallas as pl
from jax.experimental.pallas import tpu as pltpu
from jax.sharding import PartitionSpec as P

BF, F32 = jnp.bfloat16, jnp.float32
CORE = 1
BIT = {"x": 8, "y": 4, "z": 2}
ALL = (CORE, *BIT.values())
VMEM = 60 * 2**20


def dot(a, b, ca, cb):
    return lax.dot_general(a, b, (((ca,), (cb,)), ((), ())), preferred_element_type=F32)


def call(kernel, grid, ins, outs, shapes, flops, scratch=(), aliases={}, sides=(), collective_id=None, greets=()):
    several = isinstance(shapes, list)
    outs, shapes = (outs, shapes) if several else ([outs], [shapes])
    n_in, n_out, n_scratch = len(ins), len(outs), len(scratch)
    hbm = pl.BlockSpec(memory_space=pl.ANY)
    arrays = [array for side in sides for array in side.arrays]
    results = [one for side in sides for one in side.results()]
    more = [side.scratch() for side in sides]

    def whole(*refs):
        take = iter(refs)

        def some(n):
            return [next(take) for _ in range(n)]

        main = some(n_in)
        given = [some(len(side.arrays)) for side in sides]
        main += some(n_out)
        made = [some(len(side.results())) for side in sides]
        main += some(n_scratch)
        running = [
            side.bind(given[k], made[k], some(len(more[k]))) for k, side in enumerate(sides)
        ]
        step = pl.program_id(0)
        if greets:

            @pl.when(step == 0)
            def _():
                greet(greets)

        for at in sorted({at for side in sides for at, _ in side.plan}):

            @pl.when(step == at)
            def _():
                for side, one in zip(sides, running, strict=True):
                    for when, part in side.plan:
                        if when == at:
                            one.run(part)

        kernel(*main)
        if sides:

            @pl.when(step == grid[0] - 1)
            def _():
                for one in running:
                    one.end()

    out = pl.pallas_call(
        whole,
        grid=grid,
        in_specs=[*ins, *[hbm] * len(arrays)],
        out_specs=[*outs, *[spec for spec, _ in results]],
        out_shape=[*shapes, *[shape for _, shape in results]],
        scratch_shapes=[*scratch, *[one for group in more for one in group]],
        input_output_aliases=aliases,
        cost_estimate=pl.CostEstimate(flops=flops, bytes_accessed=flops // 400, transcendentals=0),
        compiler_params=pltpu.CompilerParams(
            vmem_limit_bytes=VMEM,
            dimension_semantics=("arbitrary",) * len(grid),
            collective_id=collective_id,
            has_side_effects=bool(greets),
        ),
    )

    def run(*args):
        got = out(*args, *arrays)
        return got if several or sides else got[0]

    return run


def size(part):
    return part.stop - part.start


def like(*shapes):
    return [jax.ShapeDtypeStruct(s, d) for s, d in shapes]


def scale_of(wide):
    return lax.rsqrt(jnp.mean(wide**2, -1, keepdims=True) + 1e-6)


def normed(h):
    wide = h.astype(F32)
    return (wide * scale_of(wide)).astype(BF)


def forward(a, w_gate, w_up, n, tile=512):
    t, d = a.shape
    ff = w_gate.shape[2]

    def kernel(a, wg, wu, gate, up, hid):
        g = dot(a[...], wg[...], 1, 0)
        u = dot(a[...], wu[...], 1, 0)
        gate[...] = g
        up[...] = u
        hid[...] = (g * sigmoid(g) * u).astype(BF)

    w = pl.BlockSpec((None, d, tile), lambda j: (n, 0, j))
    o = pl.BlockSpec((t, tile), lambda j: (0, j))
    return call(
        kernel,
        (ff // tile,),
        [pl.BlockSpec((t, d), lambda j: (0, 0)), w, w],
        [o, o, o],
        like(((t, ff), F32), ((t, ff), F32), ((t, ff), BF)),
        4 * t * d * ff,
    )(a, w_gate, w_up)


def down(x, hid, w_down, n, tile=512):
    t, d = x.shape
    ff = hid.shape[1]

    def kernel(x, hid, w, h, a):
        new = x[...].astype(F32) + dot(hid[...], w[...], 1, 0).astype(BF).astype(F32)
        new = new.astype(BF)
        h[...] = new
        a[...] = normed(new)

    o = pl.BlockSpec((tile, d), lambda i: (i, 0))
    return call(
        kernel,
        (t // tile,),
        [o, pl.BlockSpec((tile, ff), lambda i: (i, 0)), pl.BlockSpec((None, ff, d), lambda i: (n, 0, 0))],
        [o, o],
        like(((t, d), BF), ((t, d), BF)),
        2 * t * d * ff,
    )(x, hid, w_down)


def sigmoid(x):
    return 0.5 * jnp.tanh(0.5 * x) + 0.5


def gated_back(g, u, d_hid):
    d_hid = d_hid.astype(BF).astype(F32)
    s = sigmoid(g)
    act = g * s
    d_up = (d_hid * act).astype(BF)
    d_gate = (d_hid * u * (s + act * (1 - s))).astype(BF)
    return act, d_gate, d_up


def turn(a, back, w_gate, w_up, w_down, n, tile=256):
    t, d = a.shape
    ff = w_gate.shape[2]

    def kernel(a, back, wg, wu, wd, hid, d_gate, d_up):
        for r in range(0, t, 512):
            r = slice(r, r + 512)
            g = dot(a[r], wg[...], 1, 0)
            u = dot(a[r], wu[...], 1, 0)
            act, d_gate[r], d_up[r] = gated_back(g, u, dot(back[r], wd[...], 1, 1))
            hid[r] = (act * u).astype(BF)

    whole = pl.BlockSpec((t, d), lambda j: (0, 0))
    w = pl.BlockSpec((None, d, tile), lambda j: (n, 0, j))
    o = pl.BlockSpec((t, tile), lambda j: (0, j))
    return call(
        kernel,
        (ff // tile,),
        [whole, whole, w, w, pl.BlockSpec((None, tile, d), lambda j: (n, j, 0))],
        [o, o, o],
        like(*[((t, ff), BF)] * 3),
        6 * t * d * ff,
    )(a, back, w_gate, w_up, w_down)


def backward(back, gate, up, w_down, n, tile=256, sides=(), collective_id=None):
    t, d = back.shape
    ff = gate.shape[1]

    def kernel(back, wd, g, u, d_gate, d_up):
        for r in range(0, t, 512):
            r = slice(r, r + 512)
            _, d_gate[r], d_up[r] = gated_back(g[r], u[r], dot(back[r], wd[...], 1, 1))

    o = pl.BlockSpec((t, tile), lambda j: (0, j))
    return call(
        kernel,
        (ff // tile,),
        [once((t, d), lambda j: (0, 0)), pl.BlockSpec((None, tile, d), lambda j: (n, j, 0)), o, o],
        [o, o],
        like(*[((t, ff), BF)] * 2),
        2 * t * d * ff,
        sides=sides,
        greets=ALL,
        collective_id=collective_id,
    )(back, w_down, gate, up)


def through(d_gate, d_up, w_gate, w_up, h, back, n, tile=256, sides=(), collective_id=None):
    t, d = h.shape
    ff = d_gate.shape[1]

    def kernel(dg, du, wg, wu, h, back, out):
        d_a = dot(dg[...], wg[...], 1, 1).astype(BF).astype(F32) + dot(du[...], wu[...], 1, 1).astype(BF).astype(F32)
        d_a = d_a.astype(BF).astype(F32)
        wide = h[...].astype(F32)
        scale = scale_of(wide)
        along = jnp.mean(d_a * wide, -1, keepdims=True)
        d_h = scale * d_a - wide * (scale**3 * along)
        out[...] = (back[...].astype(F32) + d_h.astype(BF).astype(F32)).astype(BF)

    o = pl.BlockSpec((tile, d), lambda i: (i, 0))
    wide = pl.BlockSpec((tile, ff), lambda i: (i, 0))
    w = once((None, d, ff), lambda i: (n, 0, 0))
    return call(
        kernel,
        (t // tile,),
        [wide, wide, w, w, o, o],
        o,
        like(((t, d), BF))[0],
        4 * t * d * ff,
        sides=sides,
        greets=ALL,
        collective_id=collective_id,
    )(d_gate, d_up, w_gate, w_up, h, back)


def once(shape, index):
    return pl.BlockSpec(shape, index, pipeline_mode=pl.Buffered(1))


class Crossing:
    def __init__(self, steps, slots, sent, came):
        self.steps, self.slots, self.sems = steps, slots, (sent, came)

    @staticmethod
    def scratch(steps, shape):
        sems = pltpu.SemaphoreType.DMA((steps,))
        return [pltpu.VMEM((2, *shape), BF), sems, sems]

    def copy(self, at, dst):
        return remote(self.slots.at[at % 2], dst, self.sems, at, CORE)

    def slot(self, step, dst):
        @pl.when(step >= 2)
        def _():
            self.copy(step - 2, dst).wait_send()

        return self.slots.at[step % 2]

    def end(self, step, dst):
        @pl.when(step == self.steps - 1)
        def _():
            for at in range(self.steps):
                if at >= self.steps - 2:
                    self.copy(at, dst).wait_send()
                self.copy(at, dst).wait_recv()


def by_columns(a, bs, tile=512, sides=(), collective_id=None):
    t, d = a.shape
    ff = bs[0].shape[1]
    rows, steps = d // 16, ff // tile
    total = steps * len(bs)

    def kernel(a, *refs):
        ins, refs = refs[: len(bs)], refs[len(bs) :]
        kept, got, (acc, *rest) = refs[: len(bs)], refs[len(bs) : 2 * len(bs)], refs[2 * len(bs) :]
        crossing = Crossing(total, *rest)
        me, step = lax.axis_index("dp"), pl.program_id(0)
        slot = crossing.slot(step, got[0].at[:, :, pl.ds(0, tile)])
        for k in range(len(bs)):

            @pl.when(step // steps == k)
            def _():
                acc[...] = dot(a[...], ins[k][...], 0, 0).reshape(acc.shape)
                for j in range(8):
                    slot[j] = acc[(2 * j + 1) ^ me].astype(BF)
                for j in range(8):
                    kept[k][j] = acc[(2 * j) ^ me].astype(BF)
                cols = pl.ds(pl.multiple_of((step - k * steps) * tile, tile), tile)
                crossing.copy(step, got[k].at[:, :, cols]).start()

        crossing.end(step, got[0].at[:, :, pl.ds(0, tile)])

    def at(k):
        return lambda i: jnp.clip(i - k * steps, 0, steps - 1)

    ins = [pl.BlockSpec((t, tile), lambda i, k=k: (0, at(k)(i))) for k in range(len(bs))]
    outs = [pl.BlockSpec((8, rows, tile), lambda i, k=k: (0, 0, at(k)(i))) for k in range(len(bs))]
    return call(
        kernel,
        (total,),
        [once((t, d), lambda i: (0, 0)), *ins],
        [*outs, *[pl.BlockSpec(memory_space=pl.ANY)] * len(bs)],
        like(*[((8, rows, ff), BF)] * (2 * len(bs))),
        2 * t * d * ff * len(bs),
        scratch=[pltpu.VMEM((16, rows, tile), F32), *Crossing.scratch(total, (8, rows, tile))],
        sides=sides,
        collective_id=collective_id,
        greets=ALL,
    )(a, *bs)


def by_rows(a, b, collective_id):
    t, ff = a.shape
    d = b.shape[1]
    rows = ff // 16

    def kernel(a, b, keep, got, acc, *rest):
        crossing = Crossing(4, *rest)
        me, step = lax.axis_index("dp"), pl.program_id(0)
        slot = crossing.slot(step, got.at[pl.ds(0, 2)])
        acc[...] = dot(a[...], b[...], 0, 0).reshape(acc.shape)
        low = me & 3
        for j in range(2):
            slot[j] = acc[(2 * j + 1) ^ low].astype(BF)
        for j in range(2):
            keep[j] = acc[(2 * j) ^ low].astype(BF)
        crossing.copy(step, got.at[pl.ds(2 * (step ^ (me >> 2)), 2)]).start()
        crossing.end(step, got.at[pl.ds(0, 2)])

    return call(
        kernel,
        (4,),
        [pl.BlockSpec((t, ff // 4), lambda i: (0, i)), once((t, d), lambda i: (0, 0))],
        [pl.BlockSpec((2, rows, d), lambda i: (i ^ (lax.axis_index("dp") >> 2), 0, 0)), pl.BlockSpec(memory_space=pl.ANY)],
        like(*[((8, rows, d), BF)] * 2),
        2 * t * d * ff,
        scratch=[pltpu.VMEM((4, rows, d), F32), *Crossing.scratch(4, (2, rows, d))],
        collective_id=collective_id,
        greets=(CORE,),
    )(a, b)


def placed(parts, pieces, last):
    shapes = [(8, 2, cut[-1][0].stop, cut[-1][1].stop) for cut in pieces]
    last = [one.reshape(shape) for one, shape in zip(last, shapes, strict=True)]

    def kernel(*refs):
        came, went = refs[-2:]
        me = lax.axis_index("dp")
        core, pair = me & 1, me >> 1

        def copies(which, j):
            held = refs[15 + which]
            bits = {"x": j >> 2, "y": (j >> 1) & 1, "z": j & 1}
            for i, (rows, cols, order) in enumerate(pieces[which]):
                at = bits[order[0]] * 4 + bits[order[1]] * 2 + bits[order[2]]
                for side in range(2):
                    src = refs[3 * which + i].at[8 * side + at]
                    dst = held.at[pair ^ j, core ^ side, rows, cols]
                    yield pltpu.make_async_copy(src, dst, came.at[which, j, 2 * i + side])

        def leave(which, j):
            k = pair ^ j
            return pltpu.make_async_copy(refs[15 + which].at[k], refs[12 + which].at[0, k], went.at[which, j])

        into = [pltpu.make_async_copy(refs[9 + k], refs[18 + k], came.at[k, 8, 0]) for k in range(3)]
        off = [pltpu.make_async_copy(refs[18 + k], refs[12 + k].at[1], went.at[k, 8]) for k in range(3)]
        for which in range(3):
            into[which].start()
        for which in range(3):
            for j in range(8):
                for copy in copies(which, j):
                    copy.start()
        for which in range(3):
            into[which].wait()
            off[which].start()
        for which in range(3):
            for j in range(8):
                for copy in copies(which, j):
                    copy.wait()
                leave(which, j).start()
        for which in range(3):
            off[which].wait()
            for j in range(8):
                leave(which, j).wait()

    whole = pl.BlockSpec(memory_space=pl.ANY)
    return list(
        pl.pallas_call(
            kernel,
            in_specs=[whole] * 12,
            out_specs=[whole] * 3,
            out_shape=like(*[((2, *shape), BF) for shape in shapes]),
            scratch_shapes=[
                *[pltpu.VMEM(shape, BF) for shape in shapes] * 2,
                pltpu.SemaphoreType.DMA((3, 9, 6)),
                pltpu.SemaphoreType.DMA((3, 9)),
            ],
            cost_estimate=pl.CostEstimate(flops=10**9, bytes_accessed=10**7, transcendentals=0),
            compiler_params=pltpu.CompilerParams(vmem_limit_bytes=VMEM),
            name="placed",
        )(*parts[0], *parts[1], *parts[2], *last)
    )


BITS = {"x": 4, "y": 2, "z": 1}


def peer(bit):
    return {"dp": lax.axis_index("dp") ^ bit}


def remote(src, dst, sems, i, bit):
    return pltpu.make_async_remote_copy(
        src, dst, sems[0].at[i], sems[1].at[i], device_id=peer(bit), device_id_type=pl.DeviceIdType.MESH
    )


def greet(bits):
    barrier = pltpu.get_barrier_semaphore()
    for bit in bits:
        pl.semaphore_signal(barrier, inc=1, device_id=peer(bit), device_id_type=pl.DeviceIdType.MESH)
    pl.semaphore_wait(barrier, len(bits))


class Summed:
    def __init__(self, pieces, refs):
        self.pieces = pieces
        self.mine, self.other = refs[:2]
        self.out = [refs[2 + 3 * i : 5 + 3 * i] for i in range(3)]
        self.got = [refs[11 + 3 * i : 14 + 3 * i] for i in range(3)]
        self.sems = refs[20:22]

    @staticmethod
    def scratch(pieces, shape):
        whole = [pltpu.VMEM((8, *shape), BF)] * 2
        halves = [pltpu.VMEM((n, size(rows), size(cols)), BF) for rows, cols, _ in pieces for n in (4, 2, 1)]
        return [*whole, *halves, *halves, pltpu.SemaphoreType.DMA((9,)), pltpu.SemaphoreType.DMA((9,))]

    def copy(self, i, stage):
        return remote(self.out[i][stage], self.got[i][stage], self.sems, 3 * i + stage, BIT[self.pieces[i][2][stage]])

    def term(self, i, stage, j):
        rows, cols, order = self.pieces[i]
        total = self.mine[j, rows, cols].astype(F32) + self.other[j, rows, cols].astype(F32)
        for past in range(stage):
            total = total + self.got[i][past][self.place(order, past, j)].astype(F32)
        return total

    @staticmethod
    def place(order, stage, j):
        rest = [axis for axis in "xyz" if axis not in order[: stage + 1]]
        return sum(bool(j & BITS[axis]) << (len(rest) - 1 - k) for k, axis in enumerate(rest))

    def send(self, stage, i):
        order = self.pieces[i][2]
        if stage:
            self.copy(i, stage - 1).wait_recv()
        for j in range(8):
            gone = any(j & BITS[axis] for axis in order[:stage])
            if j & BITS[order[stage]] and not gone:
                self.out[i][stage][self.place(order, stage, j)] = self.term(i, stage, j).astype(BF)
        self.copy(i, stage).start()

    def total(self, i):
        self.copy(i, 2).wait_recv()
        return self.term(i, 3, 0).astype(BF).astype(F32)

    def finish(self):
        for i in range(3):
            for stage in range(3):
                self.copy(i, stage).wait_send()


class Sum:
    def __init__(self, pieces, keep, got, plan=()):
        self.pieces, self.arrays = pieces, [keep, got]
        self.shape = keep.shape[1:]
        self.plan = [(0, "load"), *[(at, (stage, i)) for stage, at in enumerate(plan) for i in range(3)]]

    def results(self):
        return [(pl.BlockSpec(self.shape, lambda i: (0, 0)), jax.ShapeDtypeStruct(self.shape, BF))]

    def scratch(self):
        return [*Summed.scratch(self.pieces, self.shape), pltpu.SemaphoreType.DMA((2,))]

    def bind(self, ins, outs, refs):
        one = Sum.__new__(Sum)
        one.pieces, one.given = self.pieces, ins
        one.out = outs[0] if outs else None
        one.sum, one.local = Summed(self.pieces, refs[:22]), refs[22]
        return one

    def copies(self):
        into = (self.sum.mine, self.sum.other)
        return [pltpu.make_async_copy(self.given[k], into[k], self.local.at[k]) for k in range(2)]

    def run(self, part):
        if part == "load":
            for copy in self.copies():
                copy.start()
            return
        stage, i = part
        if part == (0, 0):
            for copy in self.copies():
                copy.wait()
        self.sum.send(stage, i)

    def end(self):
        for i, (rows, cols, _) in enumerate(self.pieces):
            self.out[rows, cols] = self.sum.total(i).astype(BF)
        self.sum.finish()


class Spread:
    def __init__(self, pieces, block, plan=()):
        self.pieces, self.arrays, self.shape = pieces, [block], block.shape
        self.plan = list(zip(plan, ("begin", 0, 1, 2)))

    def results(self):
        return [
            (pl.BlockSpec(memory_space=pl.ANY), jax.ShapeDtypeStruct((16, size(rows), size(cols)), BF))
            for rows, cols, _ in self.pieces
        ]

    @staticmethod
    def scratch():
        return [pltpu.SemaphoreType.DMA((27,)), pltpu.SemaphoreType.DMA((27,)), pltpu.SemaphoreType.DMA((3,))]

    def bind(self, ins, outs, sems):
        own = ins if len(ins) == 3 else [ins[0].at[rows, cols] for rows, cols, _ in self.pieces]
        one = Spread.__new__(Spread)
        one.pieces, one.own, one.outs = self.pieces, own, outs
        one.sems, one.local = sems[:2], sems[2]
        return one

    def along(self, i, stage):
        out, n, bit = self.outs[i], 1 << stage, BIT[self.pieces[i][2][2 - stage]]
        copies = [remote(self.own[i], out.at[n], self.sems, 9 * i + 2 * stage, bit)]
        if stage:
            src, dst = out.at[pl.ds(1, n - 1)], out.at[pl.ds(n + 1, n - 1)]
            copies.append(remote(src, dst, self.sems, 9 * i + 2 * stage - 1, bit))
        return copies

    def across(self, i, stage):
        out, at = self.outs[i], 9 * i + 5 + stage
        if stage == 0:
            return remote(self.own[i], out.at[8], self.sems, at, CORE)
        n = 1 << (stage - 1)
        return remote(out.at[pl.ds(n, n)], out.at[pl.ds(8 + n, n)], self.sems, at, CORE)

    def keep(self, i):
        return pltpu.make_async_copy(self.own[i], self.outs[i].at[0], self.local.at[i])

    def begin(self, i):
        for copy in self.along(i, 0):
            copy.start()
        self.across(i, 0).start()
        self.keep(i).start()

    def step(self, stage, i):
        for copy in self.along(i, stage):
            copy.wait_recv()
        if stage < 2:
            for copy in self.along(i, stage + 1):
                copy.start()
        self.across(i, stage + 1).start()

    def run(self, part):
        for i in range(3):
            self.begin(i) if part == "begin" else self.step(part, i)

    def end(self):
        for i in range(3):
            self.keep(i).wait()
            for stage in range(3):
                for copy in self.along(i, stage):
                    copy.wait_send()
            for stage in range(4):
                self.across(i, stage).wait()


def tail(gate, up, states, pieces):
    rows, width = gate[0].shape[1:]

    both = [Sum(pieces[k], *(gate, up)[k]) for k in range(2)]
    ways = [Spread(pieces[k], jax.ShapeDtypeStruct((rows, width), BF)) for k in range(2)]

    def kernel(*refs):
        w_in, m_in, v_in = ((refs[4 + k], refs[7 + k]) for k in range(3))
        outs = [refs[10 + 3 * k : 13 + 3 * k] for k in range(2)]
        m_out, v_out = refs[16:18], refs[18:20]
        sums = [both[k].bind(refs[2 * k : 2 * k + 2], None, refs[20 + 23 * k : 43 + 23 * k]) for k in range(2)]
        own = [refs[66:69], refs[69:72]]
        spread = [ways[k].bind(own[k], outs[k], refs[72 + 3 * k : 75 + 3 * k]) for k in range(2)]
        greet(ALL)
        for one in sums:
            one.run("load")
        for stage in range(3):
            for one in sums:
                for i in range(3):
                    one.run((stage, i))
        for k in range(2):
            for i, (_, cols, _) in enumerate(pieces[k]):
                new, m_out[k][:, cols], v_out[k][:, cols] = adamw(
                    w_in[k][:, cols].astype(F32), m_in[k][:, cols], v_in[k][:, cols], sums[k].sum.total(i)
                )
                own[k][i][...] = new
                spread[k].begin(i)
        for stage in range(3):
            for k in range(2):
                spread[k].run(stage)
        for k in range(2):
            sums[k].sum.finish()
            spread[k].end()

    hbm, vmem = pl.BlockSpec(memory_space=pl.ANY), pl.BlockSpec(memory_space=pltpu.VMEM)
    arrays = [jax.ShapeDtypeStruct((16, rows, size(cols)), BF) for k in range(2) for _, cols, _ in pieces[k]]
    state = [jax.ShapeDtypeStruct((rows, width), F32)] * 4
    out = pl.pallas_call(
        kernel,
        in_specs=[hbm] * 4 + [vmem] * 6,
        out_specs=[hbm] * 6 + [vmem] * 4,
        out_shape=[*arrays, *state],
        scratch_shapes=[
            *both[0].scratch(),
            *both[1].scratch(),
            *[pltpu.VMEM((rows, size(cols)), BF) for k in range(2) for _, cols, _ in pieces[k]],
            *Spread.scratch() * 2,
        ],
        cost_estimate=pl.CostEstimate(flops=10**11, bytes_accessed=10**8, transcendentals=0),
        compiler_params=pltpu.CompilerParams(collective_id=1, has_side_effects=True, vmem_limit_bytes=VMEM),
        name="tail",
    )(*gate, *up, *states[0], *states[1])
    return [out[3 * k : 3 * k + 3] for k in range(2)], out[6:8], out[8:10]


def adamw(w, m, v, g):
    m = 0.9 * m + 0.1 * g
    v = 0.95 * v + 0.05 * g * g
    step = m * lax.rsqrt(v + 1e-8) + 0.1 * w
    return (w - 0.02 * step).astype(BF), m, v


def solution(mesh):
    ORDERS = ("xyz", "yzx", "zxy")

    def body(x, dy, w_gate, w_up, w_down, *moments):
        x, dy = x[0], dy[0]
        m, v = moments[:3], moments[3:]
        me = lax.axis_index("dp")
        weights = (w_gate, w_up, w_down)
        new = [[None] * 2 for _ in range(9)]

        def pieces_of(which):
            orders = [ORDERS[(which + i) % 3] for i in range(3)]
            rows, width = weights[which].shape[1] // 16, weights[which].shape[2]
            if which == 2:
                ends = [0, 80, 160, rows]
                return [(slice(ends[i], ends[i + 1]), slice(0, width), orders[i]) for i in range(3)]
            ends = [0, 1152, 2304, width]
            return [(slice(0, rows), slice(ends[i], ends[i + 1]), orders[i]) for i in range(3)]

        def state(which, n):
            rows, width = weights[which].shape[1] // 16, weights[which].shape[2]
            w = lax.dynamic_slice(weights[which], (n, me * rows, 0), (1, rows, width))[0]
            return w, m[which][n], v[which][n]

        def update(which, n, g):
            w, m1, v1 = state(which, n)
            w, new[3 + which][n], new[6 + which][n] = adamw(w.astype(F32), m1, v1, g.astype(F32))
            return w

        def everywhere(w):
            return lax.all_gather(w, "dp", axis=0, tiled=True)

        a0 = normed(x)
        gate, up, hid0 = forward(a0, w_gate, w_up, 0)
        h, a1 = down(x, hid0, w_down, 0)
        hid1, d_gate, d_up = turn(a1, dy, w_gate, w_up, w_down, 1)
        pieces = [pieces_of(which) for which in range(3)]
        down1 = by_rows(hid1, dy, 5)
        sides = [Sum(pieces[2], *down1, (1, 7, 10))]
        *both, g = by_columns(a1, (d_gate, d_up), sides=sides, collective_id=2)
        w_d1 = everywhere(update(2, 1, g))
        sides = [
            Sum(pieces[0], *both[::2], (0, 3, 6)),
            Sum(pieces[1], *both[1::2], (1, 5, 7)),
        ]
        back, g_g1, g_u1 = through(d_gate, d_up, w_gate, w_up, h, dy, 1, sides=sides, collective_id=3)
        w_g1, w_u1 = everywhere(update(0, 1, g_g1)), everywhere(update(1, 1, g_u1))
        sides = [Sum(pieces[2], *by_rows(hid0, back, 7), (1, 6, 9))]
        d_gate, d_up, g = backward(back, gate, up, w_down, 0, sides=sides, collective_id=4)
        sides = [Spread(pieces[2], update(2, 0, g), (0, 3, 7, 13))]
        *both, p0, p1, p2 = by_columns(a0, (d_gate, d_up), sides=sides, collective_id=6)
        parts, ms, vs = tail(both[::2], both[1::2], (state(0, 0), state(1, 0)), pieces)
        for which in range(2):
            new[3 + which][0], new[6 + which][0] = ms[which], vs[which]
        whole = placed([*parts, (p0, p1, p2)], pieces, (w_g1, w_u1, w_d1))
        for i in range(3):
            new[i] = whole[i].reshape(weights[i].shape)
        return tuple(one if i < 3 else jnp.stack(one) for i, one in enumerate(new))

    seq = P(("rep", "dp"), None, None)
    full = P(None, None, None)
    block = P(None, "dp", None)
    return jax.shard_map(
        body,
        mesh=mesh,
        in_specs=(seq, seq, *[full] * 3, *[block] * 6),
        out_specs=(*[P("rep", None, None)] * 3, *[P("rep", "dp", None)] * 6),
        check_vma=False,
    )
```

time: 579 us -> 548 us (0.946)
  Pallas kernels: 524 us -> 493 us
    pallas_call x1, Pallas kernels: 119 us -> 95.8 us  [tail(): pl.pallas_call(kernel, in_specs=[hbm] * 4 + [vmem] * 6, out_specs=[hbm] *...]
    pallas_call x15 -> x10, Pallas kernels: 405 us -> 397 us  [the longest x9 370 us: run(): got = out(*args, *arrays)]
  transfers between devices with their start and end apart: 4 -> 3, of which waited for: 0 -> 0; matrix products, arithmetic and copies ran while one was open for 4% -> 4% of each run, Pallas kernels for 45% -> 42%
where the time goes in v2:
time: 548 us; the launch traced here: 538 us
  Pallas kernels  493 us (90%)
  other arithmetic  22.1 us (4%)
  between operations  14.2 us (3%)
  local copies, waits for them, and re-layouts  8.49 us (2%)
    pallas_call x9, Pallas kernels, run(): got = out(*args, *arrays)  370 us
    pallas_call x1, Pallas kernels, tail(): pl.pallas_call(kernel, in_specs=[hbm] * 4 + [vmem] * 6, out_specs=[hbm] *...  95.8 us
    pallas_call x1, Pallas kernels, placed(): pl.pallas_call(kernel, in_specs=[whole] * 12, out_specs=[whole] * 3, out_...  26.8 us
    another operation x6, other arithmetic, body(): jnp.stack(one)  12.5 us
  transfers between devices with their start and end apart: 3, of which 0 were waited for; matrix products, arithmetic and copies ran while one was open for 4% of the time, Pallas kernels for 42%

profile of v2, /device:TPU:0, one launch (start us, length us, event | category | flops | bytes accessed | tf_op | source)
XLA Modules:
  0.0 538.4 jit_solution(12299332595246545523)
XLA Ops:
  7.2 0.0 all-gather.4.cloned.1.call-start
  7.2 0.0 copy-start
  7.2 3.0 fusion
  10.2 0.1 copy-done
  10.4 2.5 fusion.1.refs_0_
  12.9 40.3 %shard_map.178 = (f32[2048,3584]{1,0:T(8,128)}, f32[2048,3584]{1,0:T(8,128)}, bf16[2048,3584]{1,0:T(8,128)(2,1)}) custom-call(bf16[2048,896]{1,0:T(8,128)(2,1)} %fusion.1.refs_0_, bf16[2,896,3584]{2,1,0:T(8,128)(2,1)} %refs_2_.7, bf16[2,896,3584]{2,1,0:T(8,128)(2,1)} %refs_3_.3), custom_call_target="tpu_custom_call" | custom-call | flops 26306674688 | bytes 65766688 | tf_op jit(solution)/shard_map/pallas_call | solution.py:84
  53.1 22.5 %shard_map.179 = (bf16[2048,896]{1,0:T(8,128)(2,1)}, bf16[2048,896]{1,0:T(8,128)(2,1)}) custom-call(bf16[2048,896]{1,0:T(8,128)(2,1)} %bitcast.102, bf16[2048,3584]{1,0:T(8,128)(2,1)} %get-tuple-element.52.refs_1_.refs_0_, bf16[2,3584,896]{2,1,0:T(8,128)(2,1)} %refs_1_.3), custom_call_target="tpu_custom_call" | custom-call | flops 13153337344 | bytes 32883344 | tf_op jit(solution)/shard_map/pallas_call | solution.py:84
  75.6 54.5 %shard_map.180 = (bf16[2048,3584]{1,0:T(8,128)(2,1)}, bf16[2048,3584]{1,0:T(8,128)(2,1)}, bf16[2048,3584]{1,0:T(8,128)(2,1)}) custom-call(bf16[2048,896]{1,0:T(8,128)(2,1)} %get-tuple-element.53.refs_0_, bf16[2048,896]{1,0:T(8,128)(2,1)} %bitcast.113, bf16[2,896,3584]{2,1,0:T(8,128)(2,1)} %refs_2_.7, bf16[2,896,3584]{2,1,0:T(8,128)(2,1)} %refs_3_.3, ...), custom_call_target="tpu_custom_call" | custom-call | flops 39460012032 | bytes 98650032 | tf_op jit(solution)/shard_map/pallas_call | solution.py:84
  130.1 24.0 %shard_map.181 = (bf16[8,224,896]{2,1,0:T(8,128)(2,1)}, bf16[8,224,896]{2,1,0:T(8,128)(2,1)}) custom-call(bf16[2048,3584]{1,0:T(8,128)(2,1)} %get-tuple-element.57.refs_0_, bf16[2048,896]{1,0:T(8,128)(2,1)} %bitcast.114), custom_call_target="tpu_custom_call" | custom-call | flops 13153337344 | bytes 32883344 | tf_op jit(solution)/shard_map/pallas_call | solution.py:84
  154.1 45.1 %shard_map.182 = (bf16[8,56,3584]{2,1,0:T(8,128)(2,1)}, bf16[8,56,3584]{2,1,0:T(8,128)(2,1)}, bf16[8,56,3584]{2,1,0:T(8,128)(2,1)}, bf16[8,56,3584]{2,1,0:T(8,128)(2,1)}, bf16[224,896]{1,0:T(8,128)(2,1)}) custom-call(bf16[2048,896]{1,0:T(8,128)(2,1)} %get-tuple-element.53.refs_0_, bf16[2048,3584]{1,0:T(8,128)(2,1)} %get-tuple-element.54.refs_1_.refs_0_, ...), custom_call_target="tpu_custom_call" | custom-call | flops 26306674688 | bytes 65766688 | tf_op jit(solution)/shard_map/pallas_call | solution.py:84
  199.2 0.0 copy-start.5
  199.2 0.0 copy-start.6
  199.2 55.3 %shard_map.183 = (bf16[2048,896]{1,0:T(8,128)(2,1)}, bf16[56,3584]{1,0:T(8,128)(2,1)}, bf16[56,3584]{1,0:T(8,128)(2,1)}) custom-call(bf16[2048,3584]{1,0:T(8,128)(2,1)} %get-tuple-element.54.refs_1_.refs_0_, bf16[2048,3584]{1,0:T(8,128)(2,1)} %get-tuple-element.55.refs_2_.refs_1_, bf16[2,896,3584]{2,1,0:T(8,128)(2,1)} %refs_2_.7, ...), custom_call_target="tpu_custom_call" | custom-call | flops 26306674688 | bytes 65766688 | tf_op jit(solution)/shard_map/pallas_call | solution.py:84
  254.5 0.0 copy-done.5
  254.5 0.0 copy-done.6
  254.5 4.3 fusion.26
  258.8 0.0 all-gather.4.cloned.1.call-update
  258.8 0.0 all-gather.6.cloned.1.call-start
  258.9 0.7 all-gather.6.cloned.1.call-update
  259.6 0.0 all-gather.8.cloned.1.call-start
  259.6 23.8 %shard_map.184 = (bf16[8,224,896]{2,1,0:T(8,128)(2,1)}, bf16[8,224,896]{2,1,0:T(8,128)(2,1)}) custom-call(bf16[2048,3584]{1,0:T(8,128)(2,1)} %get-tuple-element.52.refs_1_.refs_0_, bf16[2048,896]{1,0:T(8,128)(2,1)} %get-tuple-element.64.refs_1_.refs_0_), custom_call_target="tpu_custom_call" | custom-call | flops 13153337344 | bytes 32883344 | tf_op jit(solution)/shard_map/pallas_call | solution.py:84
  283.4 0.0 copy-start.12
  283.4 55.1 %shard_map.185 = (bf16[2048,3584]{1,0:T(8,128)(2,1)}, bf16[2048,3584]{1,0:T(8,128)(2,1)}, bf16[224,896]{1,0:T(8,128)(2,1)}) custom-call(bf16[2048,896]{1,0:T(8,128)(2,1)} %get-tuple-element.64.refs_1_.refs_0_, bf16[2,3584,896]{2,1,0:T(8,128)(2,1)} %refs_1_.3, f32[2048,3584]{1,0:T(8,128)} %get-tuple-element.65.refs_2_, ...), custom_call_target="tpu_custom_call" | custom-call | flops 13153337344 | bytes 32883344 | tf_op jit(solution)/shard_map/pallas_call | solution.py:84
  338.5 0.0 copy-done.12
  338.5 4.1 fusion.17
  342.6 0.0 all-gather.8.cloned.1.call-update
  342.7 0.0 copy-start.7
  342.7 0.0 copy-start.8
  342.7 2.8 slice_bitcast_fusion.2
  345.5 0.0 copy-done.7
  345.5 0.0 copy-done.8
  345.5 1.3 slice_bitcast_fusion
  346.8 49.7 %shard_map.186 = (bf16[8,56,3584]{2,1,0:T(8,128)(2,1)}, bf16[8,56,3584]{2,1,0:T(8,128)(2,1)}, bf16[8,56,3584]{2,1,0:T(8,128)(2,1)}, bf16[8,56,3584]{2,1,0:T(8,12...) custom-call(bf16[2048,896]{1,0:T(8,128)(2,1)} %fusion.1.refs_0_, ...), custom_call_target="tpu_custom_call" | custom-call | flops 26306674688 | bytes 65766688 | tf_op jit(solution)/shard_map/pallas_call | solution.py:84
  396.5 1.8 dynamic-slice_bitcast_fusion.1.refs_4_
  398.3 1.9 pad_maximum_fusion.2
  400.2 1.8 dynamic-slice_bitcast_fusion.refs_7_
  401.9 95.8 %tail.1 = (bf16[16,56,1152]{2,1,0:T(8,128)(2,1)}, bf16[16,56,1152]{2,1,0:T(8,128)(2,1)}, bf16[16,56,1280]{2,1,0:T(8,128)(2,1)}, bf16[16,56,1152]{2,1,0:T(8,128)(...) custom-call(bf16[8,56,3584]{2,1,0:T(8,128)(2,1)} %get-tuple-element., ...), custom_call_target="tpu_custom_call" | custom-call | flops 99999997952 | bytes 100000000 | tf_op jit(solution)/shard_map/tail/pallas_call | solution.py:626
  497.8 0.0 copy-start.3
  497.8 0.0 copy-start.11
  497.8 2.5 pad_maximum_fusion
  500.3 0.0 copy-done.11
  500.4 1.3 pad_maximum_fusion.1
  501.6 0.1 copy-done.2
  501.7 0.6 copy-done.10
  502.3 1.3 pad_maximum_fusion.3
  503.6 0.0 copy-done.1
  503.6 1.3 pad_maximum_fusion.4
  504.8 26.8 %placed.1 = (bf16[2,8,2,56,3584]{4,3,2,1,0:T(8,128)(2,1)}, bf16[2,8,2,56,3584]{4,3,2,1,0:T(8,128)(2,1)}, bf16[2,8,2,224,896]{4,3,2,1,0:T(8,128)(2,1)}) custom-call(bf16[16,56,1152]{2,1,0:T(8,128)(2,1)} %get-tuple-element.76.refs_0_, bf16[16,56,1152]{2,1,0:T(8,128)(2,1)} %get-tuple-element.77.refs_1_, bf16[16,56,1280]{2,1,0:T(8,128)(2,1)} %get-tuple-element.78.refs_2_, ...), custom_call_target="tpu_custom_call" | custom-call | flops 1000000000 | bytes 10000000 | tf_op jit(solution)/shard_map/placed/pallas_call | solution.py:395
  (12 shorter events, 0.0 us)
Async XLA Ops:
  7.2 497.7 %all-gather.4.cloned.1.call-start = ((), (), s32[]{:S(2)}) async-start(), calls=%async_computation | async-start | bytes 6823936 | tf_op jit(solution)/shard_map/all_gather | solution.py:681
  7.2 3.1 copy-start
  199.2 55.4 %copy-start.5 = (f32[2,56,3584]{2,1,0:T(8,128)S(1)}, f32[2,56,3584]{2,1,0:T(8,128)}, u32[]{:S(2)}) copy-start(f32[2,56,3584]{2,1,0:T(8,128)} %param.19) | copy-start | bytes 4816900
  199.2 55.4 %copy-start.6 = (f32[2,56,3584]{2,1,0:T(8,128)S(1)}, f32[2,56,3584]{2,1,0:T(8,128)}, u32[]{:S(2)}) copy-start(f32[2,56,3584]{2,1,0:T(8,128)} %param.16) | copy-start | bytes 4816900
  258.8 246.0 %all-gather.6.cloned.1.call-start = ((), (), s32[]{:S(2)}) async-start(), calls=%async_computation.1 | async-start | bytes 6823936 | tf_op jit(solution)/shard_map/all_gather | solution.py:681
  259.6 245.3 %all-gather.8.cloned.1.call-start = ((), (), s32[]{:S(2)}) async-start(), calls=%async_computation.2 | async-start | bytes 6823936 | tf_op jit(solution)/shard_map/all_gather | solution.py:681
  283.4 55.1 %copy-start.12 = (bf16[224,896]{1,0:T(8,128)(2,1)S(1)}, bf16[224,896]{1,0:T(8,128)(2,1)}, u32[]{:S(2)}) copy-start(bf16[224,896]{1,0:T(8,128)(2,1)} %get-tuple-element.87) | copy-start | bytes 1204228
  342.7 2.8 copy-start.7
  342.7 2.8 copy-start.8
  401.9 95.9 %copy-start.4 = (f32[1,56,3584]{2,1,0:T(8,128)S(1)}, f32[1,56,3584]{2,1,0:T(8,128)}, u32[]{:S(2)}) copy-start(f32[1,56,3584]{2,1,0:T(8,128)} %get-tuple-element.107) | copy-start | bytes 2408452
  497.8 2.6 copy-start.3
  497.8 2.6 copy-start.11
  500.3 1.4 copy-start.2
  500.3 2.0 copy-start.10
  501.6 1.9 copy-start.1
  501.6 2.0 copy-start.9
Sparse Core Ops, SparseCore 0:
  258.9 45.8 all-gather.3
  307.1 46.3 all-gather.5
  355.7 49.4 all-gather.7

commit v3 on v2

--- a/solution.py
+++ b/solution.py
@@ -104,16 +104,18 @@
     return (wide * scale_of(wide)).astype(BF)
 
 
-def forward(a, w_gate, w_up, n, tile=512):
+def forward(a, w_gate, w_up, n, tile=256):
     t, d = a.shape
     ff = w_gate.shape[2]
 
     def kernel(a, wg, wu, gate, up, hid):
-        g = dot(a[...], wg[...], 1, 0)
-        u = dot(a[...], wu[...], 1, 0)
-        gate[...] = g
-        up[...] = u
-        hid[...] = (g * sigmoid(g) * u).astype(BF)
+        for r in range(0, t, 512):
+            r = slice(r, r + 512)
+            g = dot(a[r], wg[...], 1, 0)
+            u = dot(a[r], wu[...], 1, 0)
+            gate[r] = g
+            up[r] = u
+            hid[r] = (g * sigmoid(g) * u).astype(BF)
 
     w = pl.BlockSpec((None, d, tile), lambda j: (n, 0, j))
     o = pl.BlockSpec((t, tile), lambda j: (0, j))
@@ -593,7 +595,7 @@
     ways = [Spread(pieces[k], jax.ShapeDtypeStruct((rows, width), BF)) for k in range(2)]
 
     def kernel(*refs):
-        w_in, m_in, v_in = ((refs[4 + k], refs[7 + k]) for k in range(3))
+        w_in, m_in, v_in = (refs[4 + 2 * k : 6 + 2 * k] for k in range(3))
         outs = [refs[10 + 3 * k : 13 + 3 * k] for k in range(2)]
         m_out, v_out = refs[16:18], refs[18:20]
         sums = [both[k].bind(refs[2 * k : 2 * k + 2], None, refs[20 + 23 * k : 43 + 23 * k]) for k in range(2)]
@@ -620,12 +622,15 @@
             sums[k].sum.finish()
             spread[k].end()
 
-    hbm, vmem = pl.BlockSpec(memory_space=pl.ANY), pl.BlockSpec(memory_space=pltpu.VMEM)
+    hbm, vmem = pl.BlockSpec(memory_space=pl.ANY), once((rows, width), lambda i: (0, 0))
+    first = once((None, rows, width), lambda i: (0, 0, 0))
+    mine = once((None, rows, width), lambda i: (0, lax.axis_index("dp"), 0))
     arrays = [jax.ShapeDtypeStruct((16, rows, size(cols)), BF) for k in range(2) for _, cols, _ in pieces[k]]
     state = [jax.ShapeDtypeStruct((rows, width), F32)] * 4
     out = pl.pallas_call(
         kernel,
-        in_specs=[hbm] * 4 + [vmem] * 6,
+        grid=(1,),
+        in_specs=[hbm] * 4 + [mine] * 2 + [first] * 4,
         out_specs=[hbm] * 6 + [vmem] * 4,
         out_shape=[*arrays, *state],
         scratch_shapes=[
@@ -637,7 +642,7 @@
         cost_estimate=pl.CostEstimate(flops=10**11, bytes_accessed=10**8, transcendentals=0),
         compiler_params=pltpu.CompilerParams(collective_id=1, has_side_effects=True, vmem_limit_bytes=VMEM),
         name="tail",
-    )(*gate, *up, *states[0], *states[1])
+    )(*gate, *up, *[state[i] for i in range(3) for state in states])
     return [out[3 * k : 3 * k + 3] for k in range(2)], out[6:8], out[8:10]
 
 
@@ -699,7 +704,7 @@
         d_gate, d_up, g = backward(back, gate, up, w_down, 0, sides=sides, collective_id=4)
         sides = [Spread(pieces[2], update(2, 0, g), (0, 3, 7, 13))]
         *both, p0, p1, p2 = by_columns(a0, (d_gate, d_up), sides=sides, collective_id=6)
-        parts, ms, vs = tail(both[::2], both[1::2], (state(0, 0), state(1, 0)), pieces)
+        parts, ms, vs = tail(both[::2], both[1::2], [(weights[k], m[k], v[k]) for k in range(2)], pieces)
         for which in range(2):
             new[3 + which][0], new[6 + which][0] = ms[which], vs[which]
         whole = placed([*parts, (p0, p1, p2)], pieces, (w_g1, w_u1, w_d1))

time: 548 us -> 537 us (0.980)
  local copies, waits for them, and re-layouts: 8.49 us -> 0.19 us
    squeeze x4 -> x0, local copies, waits for them, and re-layouts: 7.62 us -> none  [the longest x2 4.06 us: state(): return (w, m[which][n], v[which][n])]
  transfers between devices with their start and end apart: 3 -> 3, of which waited for: 0 -> 0; matrix products, arithmetic and copies ran while one was open for 4% -> 2% of each run, Pallas kernels for 42% -> 43%
where the time goes in v3:
time: 537 us; the launch traced here: 529 us
  Pallas kernels  492 us (92%)
  other arithmetic  22.1 us (4%)
  between operations  14.2 us (3%)
    pallas_call x9, Pallas kernels, run(): got = out(*args, *arrays)  366 us
    pallas_call x1, Pallas kernels, tail(): pl.pallas_call(kernel, grid=(1,), in_specs=[hbm] * 4 + [mine] * 2 + [firs...  99.3 us
    pallas_call x1, Pallas kernels, placed(): pl.pallas_call(kernel, in_specs=[whole] * 12, out_specs=[whole] * 3, out_...  26.8 us
    another operation x6, other arithmetic, body(): jnp.stack(one)  12.5 us
  transfers between devices with their start and end apart: 3, of which 0 were waited for; matrix products, arithmetic and copies ran while one was open for 2% of the time, Pallas kernels for 43%

profile of v3, /device:TPU:0, one launch (start us, length us, event | category | flops | bytes accessed | tf_op | source)
XLA Modules:
  0.0 529.4 jit_solution(1691009365969942680)
XLA Ops:
  7.2 0.0 all-gather.4.cloned.1.call-start
  7.2 0.0 copy-start
  7.2 3.0 fusion
  10.2 0.1 copy-done
  10.4 2.5 fusion.1.refs_0_
  12.9 38.2 %shard_map.178 = (f32[2048,3584]{1,0:T(8,128)}, f32[2048,3584]{1,0:T(8,128)}, bf16[2048,3584]{1,0:T(8,128)(2,1)}) custom-call(bf16[2048,896]{1,0:T(8,128)(2,1)} %fusion.1.refs_0_, bf16[2,896,3584]{2,1,0:T(8,128)(2,1)} %refs_4_.3, bf16[2,896,3584]{2,1,0:T(8,128)(2,1)} %refs_5_.1), custom_call_target="tpu_custom_call" | custom-call | flops 26306674688 | bytes 65766688 | tf_op jit(solution)/shard_map/pallas_call | solution.py:84
  51.1 22.5 %shard_map.179 = (bf16[2048,896]{1,0:T(8,128)(2,1)}, bf16[2048,896]{1,0:T(8,128)(2,1)}) custom-call(bf16[2048,896]{1,0:T(8,128)(2,1)} %bitcast.90, bf16[2048,3584]{1,0:T(8,128)(2,1)} %get-tuple-element.52.refs_1_.refs_0_, bf16[2,3584,896]{2,1,0:T(8,128)(2,1)} %refs_1_.3), custom_call_target="tpu_custom_call" | custom-call | flops 13153337344 | bytes 32883344 | tf_op jit(solution)/shard_map/pallas_call | solution.py:84
  73.6 54.5 %shard_map.180 = (bf16[2048,3584]{1,0:T(8,128)(2,1)}, bf16[2048,3584]{1,0:T(8,128)(2,1)}, bf16[2048,3584]{1,0:T(8,128)(2,1)}) custom-call(bf16[2048,896]{1,0:T(8,128)(2,1)} %get-tuple-element.53.refs_0_, bf16[2048,896]{1,0:T(8,128)(2,1)} %bitcast.101, bf16[2,896,3584]{2,1,0:T(8,128)(2,1)} %refs_4_.3, bf16[2,896,3584]{2,1,0:T(8,128)(2,1)} %refs_5_.1, ...), custom_call_target="tpu_custom_call" | custom-call | flops 39460012032 | bytes 98650032 | tf_op jit(solution)/shard_map/pallas_call | solution.py:84
  128.1 23.9 %shard_map.181 = (bf16[8,224,896]{2,1,0:T(8,128)(2,1)}, bf16[8,224,896]{2,1,0:T(8,128)(2,1)}) custom-call(bf16[2048,3584]{1,0:T(8,128)(2,1)} %get-tuple-element.57.refs_0_, bf16[2048,896]{1,0:T(8,128)(2,1)} %bitcast.102), custom_call_target="tpu_custom_call" | custom-call | flops 13153337344 | bytes 32883344 | tf_op jit(solution)/shard_map/pallas_call | solution.py:84
  152.0 45.1 %shard_map.182 = (bf16[8,56,3584]{2,1,0:T(8,128)(2,1)}, bf16[8,56,3584]{2,1,0:T(8,128)(2,1)}, bf16[8,56,3584]{2,1,0:T(8,128)(2,1)}, bf16[8,56,3584]{2,1,0:T(8,128)(2,1)}, bf16[224,896]{1,0:T(8,128)(2,1)}) custom-call(bf16[2048,896]{1,0:T(8,128)(2,1)} %get-tuple-element.53.refs_0_, bf16[2048,3584]{1,0:T(8,128)(2,1)} %get-tuple-element.54.refs_1_.refs_0_, ...), custom_call_target="tpu_custom_call" | custom-call | flops 26306674688 | bytes 65766688 | tf_op jit(solution)/shard_map/pallas_call | solution.py:84
  197.1 0.0 copy-start.8
  197.1 0.0 copy-start.9
  197.1 55.4 %shard_map.183 = (bf16[2048,896]{1,0:T(8,128)(2,1)}, bf16[56,3584]{1,0:T(8,128)(2,1)}, bf16[56,3584]{1,0:T(8,128)(2,1)}) custom-call(bf16[2048,3584]{1,0:T(8,128)(2,1)} %get-tuple-element.54.refs_1_.refs_0_, bf16[2048,3584]{1,0:T(8,128)(2,1)} %get-tuple-element.55.refs_2_.refs_1_, bf16[2,896,3584]{2,1,0:T(8,128)(2,1)} %refs_4_.3, ...), custom_call_target="tpu_custom_call" | custom-call | flops 26306674688 | bytes 65766688 | tf_op jit(solution)/shard_map/pallas_call | solution.py:84
  252.5 0.0 copy-done.8
  252.5 0.0 copy-done.9
  252.5 4.2 fusion.26
  256.7 0.0 all-gather.4.cloned.1.call-update
  256.8 0.0 all-gather.6.cloned.1.call-start
  256.8 0.7 all-gather.6.cloned.1.call-update
  257.5 0.0 all-gather.8.cloned.1.call-start
  257.6 23.8 %shard_map.184 = (bf16[8,224,896]{2,1,0:T(8,128)(2,1)}, bf16[8,224,896]{2,1,0:T(8,128)(2,1)}) custom-call(bf16[2048,3584]{1,0:T(8,128)(2,1)} %get-tuple-element.52.refs_1_.refs_0_, bf16[2048,896]{1,0:T(8,128)(2,1)} %get-tuple-element.64.refs_1_.refs_0_), custom_call_target="tpu_custom_call" | custom-call | flops 13153337344 | bytes 32883344 | tf_op jit(solution)/shard_map/pallas_call | solution.py:84
  281.3 0.0 copy-start.10
  281.4 55.1 %shard_map.185 = (bf16[2048,3584]{1,0:T(8,128)(2,1)}, bf16[2048,3584]{1,0:T(8,128)(2,1)}, bf16[224,896]{1,0:T(8,128)(2,1)}) custom-call(bf16[2048,896]{1,0:T(8,128)(2,1)} %get-tuple-element.64.refs_1_.refs_0_, bf16[2,3584,896]{2,1,0:T(8,128)(2,1)} %refs_1_.3, f32[2048,3584]{1,0:T(8,128)} %get-tuple-element.65.refs_2_, ...), custom_call_target="tpu_custom_call" | custom-call | flops 13153337344 | bytes 32883344 | tf_op jit(solution)/shard_map/pallas_call | solution.py:84
  336.4 0.0 copy-done.10
  336.5 4.1 fusion.17
  340.6 0.0 all-gather.8.cloned.1.call-update
  340.6 47.5 %shard_map.186 = (bf16[8,56,3584]{2,1,0:T(8,128)(2,1)}, bf16[8,56,3584]{2,1,0:T(8,128)(2,1)}, bf16[8,56,3584]{2,1,0:T(8,128)(2,1)}, bf16[8,56,3584]{2,1,0:T(8,12...) custom-call(bf16[2048,896]{1,0:T(8,128)(2,1)} %fusion.1.refs_0_, ...), custom_call_target="tpu_custom_call" | custom-call | flops 26306674688 | bytes 65766688 | tf_op jit(solution)/shard_map/pallas_call | solution.py:84
  388.1 1.9 pad_maximum_fusion.2
  390.1 0.0 copy-start.4
  390.1 99.3 %tail.1 = (bf16[16,56,1152]{2,1,0:T(8,128)(2,1)}, bf16[16,56,1152]{2,1,0:T(8,128)(2,1)}, bf16[16,56,1280]{2,1,0:T(8,128)(2,1)}, bf16[16,56,1152]{2,1,0:T(8,128)(...) custom-call(bf16[8,56,3584]{2,1,0:T(8,128)(2,1)} %get-tuple-element., ...), custom_call_target="tpu_custom_call" | custom-call | flops 99999997952 | bytes 100000000 | tf_op jit(solution)/shard_map/tail/pallas_call | solution.py:630
  489.4 0.0 copy-start.3
  489.4 0.0 copy-start.7
  489.4 0.0 copy-done.4
  489.4 0.0 copy-start.2
  489.4 0.0 copy-start.6
  489.4 2.6 pad_maximum_fusion
  492.0 0.0 copy-done.3
  492.0 0.0 copy-done.7
  492.0 0.0 copy-start.1
  492.0 1.3 pad_maximum_fusion.1
  493.3 0.0 copy-done.2
  493.3 0.0 copy-done.6
  493.3 1.3 pad_maximum_fusion.3
  494.6 0.0 copy-done.1
  494.6 0.0 copy-done.5
  494.6 1.3 pad_maximum_fusion.4
  495.8 0.0 all-gather.4.cloned.1.call-done
  495.8 26.8 %placed.1 = (bf16[2,8,2,56,3584]{4,3,2,1,0:T(8,128)(2,1)}, bf16[2,8,2,56,3584]{4,3,2,1,0:T(8,128)(2,1)}, bf16[2,8,2,224,896]{4,3,2,1,0:T(8,128)(2,1)}) custom-call(bf16[16,56,1152]{2,1,0:T(8,128)(2,1)} %get-tuple-element.76.refs_0_, bf16[16,56,1152]{2,1,0:T(8,128)(2,1)} %get-tuple-element.77.refs_1_, bf16[16,56,1280]{2,1,0:T(8,128)(2,1)} %get-tuple-element.78.refs_2_, ...), custom_call_target="tpu_custom_call" | custom-call | flops 1000000000 | bytes 10000000 | tf_op jit(solution)/shard_map/placed/pallas_call | solution.py:397
  (4 shorter events, 0.0 us)
Async XLA Ops:
  7.2 488.6 %all-gather.4.cloned.1.call-start = ((), (), s32[]{:S(2)}) async-start(), calls=%async_computation | async-start | bytes 6823936 | tf_op jit(solution)/shard_map/all_gather | solution.py:686
  7.2 3.1 copy-start
  197.1 55.4 %copy-start.8 = (f32[2,56,3584]{2,1,0:T(8,128)S(1)}, f32[2,56,3584]{2,1,0:T(8,128)}, u32[]{:S(2)}) copy-start(f32[2,56,3584]{2,1,0:T(8,128)} %refs_6_.1) | copy-start | bytes 4816900
  197.1 55.4 %copy-start.9 = (f32[2,56,3584]{2,1,0:T(8,128)S(1)}, f32[2,56,3584]{2,1,0:T(8,128)}, u32[]{:S(2)}) copy-start(f32[2,56,3584]{2,1,0:T(8,128)} %refs_7_.1) | copy-start | bytes 4816900
  256.8 239.1 %all-gather.6.cloned.1.call-start = ((), (), s32[]{:S(2)}) async-start(), calls=%async_computation.1 | async-start | bytes 6823936 | tf_op jit(solution)/shard_map/all_gather | solution.py:686
  257.5 238.3 %all-gather.8.cloned.1.call-start = ((), (), s32[]{:S(2)}) async-start(), calls=%async_computation.2 | async-start | bytes 6823936 | tf_op jit(solution)/shard_map/all_gather | solution.py:686
  281.3 55.1 %copy-start.10 = (bf16[224,896]{1,0:T(8,128)(2,1)S(1)}, bf16[224,896]{1,0:T(8,128)(2,1)}, u32[]{:S(2)}) copy-start(bf16[224,896]{1,0:T(8,128)(2,1)} %get-tuple-element.87) | copy-start | bytes 1204228
  390.1 99.3 %copy-start.4 = (f32[1,56,3584]{2,1,0:T(8,128)S(1)}, f32[1,56,3584]{2,1,0:T(8,128)}, u32[]{:S(2)}) copy-start(f32[1,56,3584]{2,1,0:T(8,128)} %get-tuple-element.107) | copy-start | bytes 2408452
  489.4 2.6 copy-start.3
  489.4 2.6 copy-start.7
  489.4 3.9 copy-start.2
  489.4 3.9 copy-start.6
  492.0 2.5 copy-start.1
  492.0 2.5 copy-start.5
Sparse Core Ops, SparseCore 0:
  256.9 45.9 all-gather.3
  305.1 47.9 all-gather.5
  355.9 50.9 all-gather.7
